TPU v7x, 64 devices: a 2x2x8 block of a 4x4x8 slice. The times are simulated.
64 devices in a mesh: dp: 4 (over x, y), gp: 16 (over z, core).
Axes of the slice: x: 2, y: 2, z: 8, core: 2. Of those that a mesh axis runs over, the one named last changes fastest.
The devices are a block of a 4x4x8 slice.
Arguments:
- x_prev: float32 [65536, 227], P(('dp', 'gp')), parts along dimension 0
- x_cur: float32 [65536, 227], P(('dp', 'gp')), parts along dimension 0
- forcing: float32 [65536, 2, 5], P(('dp', 'gp')), parts along dimension 0
- grid_static: float32 [65536, 5], P(('dp', 'gp')), parts along dimension 0
- g2m_feat: float32 [65536, 4], P(('dp', 'gp')), parts along dimension 0
- m2g_feat: float32 [65536, 4], P(('dp', 'gp')), parts along dimension 0
- mesh_feat: float32 [32768, 3], P(('dp', 'gp')), parts along dimension 0
- mesh_edge_feat: float32 [32768, 6, 4], P(('dp', 'gp')), parts along dimension 0
- norm_stats: float32 [4, 227], replicated
- w_grid_in: bfloat16 [464, 512], replicated
- w_mesh_in: bfloat16 [3, 512], replicated
- w_eemb_in: bfloat16 [3, 4, 512], replicated
- w_embed_out: bfloat16 [5, 512, 512], replicated
- w_edge_in: bfloat16 [18, 1536, 512], replicated
- w_edge_out: bfloat16 [18, 512, 512], replicated
- w_node_in: bfloat16 [18, 1024, 512], replicated
- w_node_out: bfloat16 [18, 512, 512], replicated
- w_grid_self: bfloat16 [2, 512, 512], replicated
- w_out_hidden: bfloat16 [512, 512], replicated
- w_out_final: bfloat16 [512, 227], replicated
Outputs:
- output 1: float32 [65536, 227], P(('dp', 'gp')), parts along dimension 0
- output 2: float32 [65536, 227], P(('dp', 'gp')), parts along dimension 0
There are 4 independent parts. A program takes and returns all parts, laid end to end along the dimension named above; an argument that names none is the same for every part.
All inputs are finite; a program needn't handle non-finite values.
Results may differ from a plain program's by a relative error of at most 0.00827091.
Values are sent between devices in bfloat16 or wider.
A program may use at most 768 MiB of HBM per device.

v0:
```python
import jax
import jax.numpy as jnp
from jax import lax
from jax.sharding import PartitionSpec as P


def layer_norm(values):
    centre = jnp.mean(values, axis=-1, keepdims=True)
    centred = values - centre
    spread = jnp.mean(centred * centred, axis=-1, keepdims=True)
    return centred * lax.rsqrt(spread + 1e-5)


def matmul_f32(values, weight):
    return jnp.dot(values, weight, preferred_element_type=jnp.float32)


def mlp_tail(pre_act, w_second):
    hidden = jax.nn.silu(pre_act).astype(jnp.bfloat16)
    return layer_norm(matmul_f32(hidden, w_second))


def residual(base, update):
    return (base.astype(jnp.float32) + update).astype(jnp.bfloat16)


def embed_static(features, w_first, w_second):
    return mlp_tail(matmul_f32(features.astype(jnp.bfloat16), w_first), w_second).astype(jnp.bfloat16)


def solution(mesh):
    group_size = mesh.shape["gp"]
    quarter_hop = group_size // 4
    row_spec = P(("dp", "gp"))
    edge_spec = P(("dp", "gp"), None, None)
    whole = P()

    def shift_pairs(hop_count):
        return [(source, (source + hop_count) % group_size) for source in range(group_size)]

    def local_run(x_prev, x_cur, forcing, grid_static, g2m_feat, m2g_feat, mesh_feat, mesh_edge_feat, norm_stats, w_grid_in, w_mesh_in, w_eemb_in, w_embed_out, w_edge_in, w_edge_out, w_node_in, w_node_out, w_grid_self, w_out_hidden, w_out_final):
        grid_dev = x_prev.shape[0]
        mesh_dev = mesh_feat.shape[0]
        grid_ratio = grid_dev // mesh_dev
        half_shard = mesh_dev // 2
        half_rows = half_shard * grid_ratio
        latent = w_embed_out.shape[-1]
        blocks = w_edge_in.shape[0]
        mesh_lat = embed_static(mesh_feat, w_mesh_in, w_embed_out[1])
        g2m_lat = embed_static(g2m_feat, w_eemb_in[0], w_embed_out[2])
        m2g_lat = embed_static(m2g_feat, w_eemb_in[1], w_embed_out[3])
        edge_base = embed_static(mesh_edge_feat, w_eemb_in[2], w_embed_out[4])
        in_mean = norm_stats[0]
        in_std = norm_stats[1]
        diff_mean = norm_stats[2]
        diff_std = norm_stats[3]
        state_prev = x_prev
        state_cur = x_cur
        outputs = []
        for step_idx in range(2):
            features = jnp.concatenate([(state_prev - in_mean) / in_std, (state_cur - in_mean) / in_std, forcing[:, step_idx, :], grid_static], axis=1)
            grid_lat = embed_static(features, w_grid_in, w_embed_out[0])
            from_prev = lax.ppermute(grid_lat[grid_dev - half_rows:], "gp", shift_pairs(1))
            senders = jnp.concatenate([from_prev, grid_lat[:grid_dev - half_rows]], axis=0)
            w_first = w_edge_in[0]
            recv_term = matmul_f32(mesh_lat, w_first[2 * latent:])
            pre_act = matmul_f32(g2m_lat, w_first[:latent]) + matmul_f32(senders, w_first[latent:2 * latent])
            pre_act = (pre_act.reshape(mesh_dev, grid_ratio, latent) + recv_term[:, None, :]).reshape(grid_dev, latent)
            enc_edge = residual(g2m_lat, mlp_tail(pre_act, w_edge_out[0]))
            enc_sum = jnp.sum(enc_edge.reshape(mesh_dev, grid_ratio, latent), axis=1, dtype=jnp.float32).astype(jnp.bfloat16)
            node_w = w_node_in[0]
            mesh_cur = residual(mesh_lat, mlp_tail(matmul_f32(mesh_lat, node_w[:latent]) + matmul_f32(enc_sum, node_w[latent:]), w_node_out[0]))
            grid_cur = residual(grid_lat, mlp_tail(matmul_f32(grid_lat, w_grid_self[0]), w_grid_self[1]))
            edge_lat = edge_base
            for layer_idx in range(1, blocks - 1):
                prev_tail = lax.ppermute(mesh_cur[mesh_dev - half_shard:], "gp", shift_pairs(1))
                next_head = lax.ppermute(mesh_cur[:half_shard], "gp", shift_pairs(-1))
                far_plus = lax.ppermute(mesh_cur, "gp", shift_pairs(-quarter_hop))
                far_minus = lax.ppermute(mesh_cur, "gp", shift_pairs(quarter_hop))
                w_layer = w_edge_in[layer_idx]
                extended = jnp.concatenate([prev_tail, mesh_cur, next_head, far_plus, far_minus], axis=0)
                send_proj = matmul_f32(extended, w_layer[latent:2 * latent])
                send_term = jnp.stack([
                    send_proj[half_shard + 1:half_shard + 1 + mesh_dev],
                    send_proj[half_shard - 1:half_shard - 1 + mesh_dev],
                    send_proj[2 * half_shard:2 * half_shard + mesh_dev],
                    send_proj[:mesh_dev],
                    send_proj[2 * mesh_dev:3 * mesh_dev],
                    send_proj[3 * mesh_dev:4 * mesh_dev]], axis=1)
                recv_term = matmul_f32(mesh_cur, w_layer[2 * latent:])
                pre_act = jnp.einsum("nkc,cd->nkd", edge_lat, w_layer[:latent], preferred_element_type=jnp.float32) + send_term + recv_term[:, None, :]
                edge_lat = residual(edge_lat, mlp_tail(pre_act, w_edge_out[layer_idx]))
                edge_sum = jnp.sum(edge_lat, axis=1, dtype=jnp.float32).astype(jnp.bfloat16)
                node_w = w_node_in[layer_idx]
                mesh_cur = residual(mesh_cur, mlp_tail(matmul_f32(mesh_cur, node_w[:latent]) + matmul_f32(edge_sum, node_w[latent:]), w_node_out[layer_idx]))
            head_next = lax.ppermute(mesh_cur[:half_shard], "gp", shift_pairs(-1))
            mesh_send = jnp.concatenate([mesh_cur[half_shard:], head_next], axis=0)
            w_last = w_edge_in[blocks - 1]
            send_term = matmul_f32(mesh_send, w_last[latent:2 * latent])
            pre_act = matmul_f32(m2g_lat, w_last[:latent]) + matmul_f32(grid_cur, w_last[2 * latent:])
            pre_act = (pre_act.reshape(mesh_dev, grid_ratio, latent) + send_term[:, None, :]).reshape(grid_dev, latent)
            dec_edge = residual(m2g_lat, mlp_tail(pre_act, w_edge_out[blocks - 1]))
            node_w = w_node_in[blocks - 1]
            grid_out = residual(grid_cur, mlp_tail(matmul_f32(grid_cur, node_w[:latent]) + matmul_f32(dec_edge, node_w[latent:]), w_node_out[blocks - 1]))
            hidden = jax.nn.silu(matmul_f32(grid_out, w_out_hidden)).astype(jnp.bfloat16)
            prediction = matmul_f32(hidden, w_out_final)
            state_next = state_cur + diff_std * prediction + diff_mean
            outputs.append(state_next)
            state_prev, state_cur = state_cur, state_next
        return outputs[0], outputs[1]

    in_specs = (row_spec, row_spec, edge_spec, row_spec, row_spec, row_spec, row_spec, edge_spec, whole) + (whole,) * 11
    return jax.shard_map(local_run, mesh=mesh, in_specs=in_specs, out_specs=(row_spec, row_spec), check_vma=False)
```

profile of v0, /device:TPU:21, one launch (start us, length us, event | category | flops | bytes accessed | tf_op | source)
XLA Modules:
  0.0 2308.9 jit_solution(4727798650599762631)
XLA Ops:
  33.6 7.1 fusion.1434
  66.0 7.8 fusion.811
  104.6 20.7 collective-permute-done.1
  158.9 18.0 collective-permute-done.5
  190.7 11.0 fusion.1443
  226.2 17.2 collective-permute-done.9
  256.8 11.0 fusion.1449
  293.3 17.3 collective-permute-done.13
  323.9 11.0 fusion.1455
  360.0 17.3 collective-permute-done.17
  390.7 11.0 fusion.1461
  426.9 17.5 collective-permute-done.21
  457.7 10.9 fusion.1467
  493.8 17.3 collective-permute-done.25
  524.5 11.0 fusion.1473
  560.6 17.3 collective-permute-done.29
  591.3 11.0 fusion.1479
  627.5 17.3 collective-permute-done.33
  658.1 11.0 fusion.1485
  694.5 17.3 collective-permute-done.37
  725.2 11.0 fusion.1491
  761.3 17.3 collective-permute-done.41
  792.0 11.1 fusion.1497
  828.2 17.3 collective-permute-done.45
  858.8 11.0 fusion.1503
  895.2 17.4 collective-permute-done.49
  925.9 11.0 fusion.1509
  962.0 17.4 collective-permute-done.53
  992.7 11.1 fusion.1515
  1029.0 17.4 collective-permute-done.57
  1059.7 11.1 fusion.1521
  1095.1 18.4 collective-permute-done.61
  1126.9 10.9 fusion.1527
  1233.3 15.3 collective-permute-done.67
  1285.4 16.7 collective-permute-done.71
  1315.5 10.9 fusion.1557
  1352.3 17.1 collective-permute-done.75
  1382.7 11.0 fusion.1563
  1419.1 17.3 collective-permute-done.79
  1449.8 10.9 fusion.1569
  1486.1 17.3 collective-permute-done.83
  1516.8 11.0 fusion.1575
  1552.7 17.5 collective-permute-done.87
  1583.6 11.0 fusion.1581
  1619.5 17.4 collective-permute-done.91
  1650.2 10.9 fusion.1587
  1686.4 17.4 collective-permute-done.95
  1717.2 10.9 fusion.1593
  1753.0 17.4 collective-permute-done.99
  1783.8 11.0 fusion.1599
  1819.8 17.4 collective-permute-done.103
  1850.5 10.9 fusion.1605
  1886.7 17.3 collective-permute-done.107
  1917.4 10.9 fusion.1611
  1953.3 17.4 collective-permute-done.111
  1984.1 11.0 fusion.1617
  2020.1 17.3 collective-permute-done.115
  2050.8 11.0 fusion.1623
  2087.0 17.4 collective-permute-done.119
  2117.7 11.0 fusion.1629
  2153.7 17.3 collective-permute-done.123
  2184.4 11.0 fusion.1635
  2219.4 18.4 collective-permute-done.127
  2251.1 10.9 fusion.1641
  (1291 shorter events, 1402.6 us)
Async XLA Ops:
  11.7 62.1 %collective-permute-start = (bf16[512,512]{0,1:T(8,128)(2,1)}, bf16[512,512]{0,1:T(8,128)(2,1)}, u32[]{:S(2)}, u32[]{:S(2)}) collective-permute-start(bf16[512,512]{0,1:T(8,128)(2,1)} %get-tuple-element.64), channel_id=1, source_target_pairs={{0,1},{1,2},{2,3},{3,4},{4,5},{5,6},{6,7},{7,8},{8,9},{9,10},{10,1... | collective-permute-start | bytes 1572872 | tf_op jit(solution)/shard_map/ppermute | solution.py:63
  93.7 32.4 %collective-permute-start.3 = (bf16[512,512]{1,0:T(8,128)(2,1)S(1)}, bf16[512,512]{1,0:T(8,128)(2,1)S(1)}, u32[]{:S(2)}, u32[]{:S(2)}) collective-permute-start(bf16[512,512]{1,0:T(8,128)(2,1)S(1)} %fusion.113), channel_id=1, source_target_pairs={{0,12},{1,13},{2,14},{3,15},{4,0},{5,1},{6,2},{7,3},{8,4},{9,5},{1... | collective-permute-start | bytes 1572872 | tf_op jit(solution)/shard_map/ppermute | solution.py:78
  100.1 26.7 %collective-permute-start.4 = (bf16[512,512]{1,0:T(8,128)(2,1)S(1)}, bf16[512,512]{1,0:T(8,128)(2,1)S(1)}, u32[]{:S(2)}, u32[]{:S(2)}) collective-permute-start(bf16[512,512]{1,0:T(8,128)(2,1)S(1)} %fusion.113), channel_id=1, source_target_pairs={{0,4},{1,5},{2,6},{3,7},{4,8},{5,9},{6,10},{7,11},{8,12},{9,13},{1... | collective-permute-start | bytes 1572872 | tf_op jit(solution)/shard_map/ppermute | solution.py:79
  149.4 30.3 %collective-permute-start.7 = (bf16[512,512]{1,0:T(8,128)(2,1)S(1)}, bf16[512,512]{1,0:T(8,128)(2,1)S(1)}, u32[]{:S(2)}, u32[]{:S(2)}) collective-permute-start(bf16[512,512]{1,0:T(8,128)(2,1)S(1)} %add_convert_fusion.75), channel_id=1, source_target_pairs={{0,12},{1,13},{2,14},{3,15},{4,0},{5,1},{6,2},{7,3},{8,4},{9,5},{1... | collective-permute-start | bytes 1572872 | tf_op jit(solution)/shard_map/ppermute | solution.py:78
  151.7 28.8 %collective-permute-start.8 = (bf16[512,512]{1,0:T(8,128)(2,1)S(1)}, bf16[512,512]{1,0:T(8,128)(2,1)S(1)}, u32[]{:S(2)}, u32[]{:S(2)}) collective-permute-start(bf16[512,512]{1,0:T(8,128)(2,1)S(1)} %add_convert_fusion.75), channel_id=1, source_target_pairs={{0,4},{1,5},{2,6},{3,7},{4,8},{5,9},{6,10},{7,11},{8,12},{9,13},{1... | collective-permute-start | bytes 1572872 | tf_op jit(solution)/shard_map/ppermute | solution.py:79
  214.7 31.1 %collective-permute-start.11 = (bf16[512,512]{1,0:T(8,128)(2,1)S(1)}, bf16[512,512]{1,0:T(8,128)(2,1)S(1)}, u32[]{:S(2)}, u32[]{:S(2)}) collective-permute-start(bf16[512,512]{1,0:T(8,128)(2,1)S(1)} %add_convert_fusion.74), channel_id=1, source_target_pairs={{0,12},{1,13},{2,14},{3,15},{4,0},{5,1},{6,2},{7,3},{8,4},{9,5},{1... | collective-permute-start | bytes 1572872 | tf_op jit(solution)/shard_map/ppermute | solution.py:78
  218.3 28.2 %collective-permute-start.12 = (bf16[512,512]{1,0:T(8,128)(2,1)S(1)}, bf16[512,512]{1,0:T(8,128)(2,1)S(1)}, u32[]{:S(2)}, u32[]{:S(2)}) collective-permute-start(bf16[512,512]{1,0:T(8,128)(2,1)S(1)} %add_convert_fusion.74), channel_id=1, source_target_pairs={{0,4},{1,5},{2,6},{3,7},{4,8},{5,9},{6,10},{7,11},{8,12},{9,13},{1... | collective-permute-start | bytes 1572872 | tf_op jit(solution)/shard_map/ppermute | solution.py:79
  280.7 32.1 %collective-permute-start.15 = (bf16[512,512]{1,0:T(8,128)(2,1)S(1)}, bf16[512,512]{1,0:T(8,128)(2,1)S(1)}, u32[]{:S(2)}, u32[]{:S(2)}) collective-permute-start(bf16[512,512]{1,0:T(8,128)(2,1)S(1)} %add_convert_fusion.73), channel_id=1, source_target_pairs={{0,12},{1,13},{2,14},{3,15},{4,0},{5,1},{6,2},{7,3},{8,4},{9,5},{1... | collective-permute-start | bytes 1572872 | tf_op jit(solution)/shard_map/ppermute | solution.py:78
  285.2 28.5 %collective-permute-start.16 = (bf16[512,512]{1,0:T(8,128)(2,1)S(1)}, bf16[512,512]{1,0:T(8,128)(2,1)S(1)}, u32[]{:S(2)}, u32[]{:S(2)}) collective-permute-start(bf16[512,512]{1,0:T(8,128)(2,1)S(1)} %add_convert_fusion.73), channel_id=1, source_target_pairs={{0,4},{1,5},{2,6},{3,7},{4,8},{5,9},{6,10},{7,11},{8,12},{9,13},{1... | collective-permute-start | bytes 1572872 | tf_op jit(solution)/shard_map/ppermute | solution.py:79
  347.9 31.8 %collective-permute-start.19 = (bf16[512,512]{1,0:T(8,128)(2,1)S(1)}, bf16[512,512]{1,0:T(8,128)(2,1)S(1)}, u32[]{:S(2)}, u32[]{:S(2)}) collective-permute-start(bf16[512,512]{1,0:T(8,128)(2,1)S(1)} %add_convert_fusion.72), channel_id=1, source_target_pairs={{0,12},{1,13},{2,14},{3,15},{4,0},{5,1},{6,2},{7,3},{8,4},{9,5},{1... | collective-permute-start | bytes 1572872 | tf_op jit(solution)/shard_map/ppermute | solution.py:78
  352.2 28.2 %collective-permute-start.20 = (bf16[512,512]{1,0:T(8,128)(2,1)S(1)}, bf16[512,512]{1,0:T(8,128)(2,1)S(1)}, u32[]{:S(2)}, u32[]{:S(2)}) collective-permute-start(bf16[512,512]{1,0:T(8,128)(2,1)S(1)} %add_convert_fusion.72), channel_id=1, source_target_pairs={{0,4},{1,5},{2,6},{3,7},{4,8},{5,9},{6,10},{7,11},{8,12},{9,13},{1... | collective-permute-start | bytes 1572872 | tf_op jit(solution)/shard_map/ppermute | solution.py:79
  414.7 32.0 %collective-permute-start.23 = (bf16[512,512]{1,0:T(8,128)(2,1)S(1)}, bf16[512,512]{1,0:T(8,128)(2,1)S(1)}, u32[]{:S(2)}, u32[]{:S(2)}) collective-permute-start(bf16[512,512]{1,0:T(8,128)(2,1)S(1)} %add_convert_fusion.71), channel_id=1, source_target_pairs={{0,12},{1,13},{2,14},{3,15},{4,0},{5,1},{6,2},{7,3},{8,4},{9,5},{1... | collective-permute-start | bytes 1572872 | tf_op jit(solution)/shard_map/ppermute | solution.py:78
  419.0 28.5 %collective-permute-start.24 = (bf16[512,512]{1,0:T(8,128)(2,1)S(1)}, bf16[512,512]{1,0:T(8,128)(2,1)S(1)}, u32[]{:S(2)}, u32[]{:S(2)}) collective-permute-start(bf16[512,512]{1,0:T(8,128)(2,1)S(1)} %add_convert_fusion.71), channel_id=1, source_target_pairs={{0,4},{1,5},{2,6},{3,7},{4,8},{5,9},{6,10},{7,11},{8,12},{9,13},{1... | collective-permute-start | bytes 1572872 | tf_op jit(solution)/shard_map/ppermute | solution.py:79
  481.6 31.9 %collective-permute-start.27 = (bf16[512,512]{1,0:T(8,128)(2,1)S(1)}, bf16[512,512]{1,0:T(8,128)(2,1)S(1)}, u32[]{:S(2)}, u32[]{:S(2)}) collective-permute-start(bf16[512,512]{1,0:T(8,128)(2,1)S(1)} %add_convert_fusion.70), channel_id=1, source_target_pairs={{0,12},{1,13},{2,14},{3,15},{4,0},{5,1},{6,2},{7,3},{8,4},{9,5},{1... | collective-permute-start | bytes 1572872 | tf_op jit(solution)/shard_map/ppermute | solution.py:78
  485.7 28.5 %collective-permute-start.28 = (bf16[512,512]{1,0:T(8,128)(2,1)S(1)}, bf16[512,512]{1,0:T(8,128)(2,1)S(1)}, u32[]{:S(2)}, u32[]{:S(2)}) collective-permute-start(bf16[512,512]{1,0:T(8,128)(2,1)S(1)} %add_convert_fusion.70), channel_id=1, source_target_pairs={{0,4},{1,5},{2,6},{3,7},{4,8},{5,9},{6,10},{7,11},{8,12},{9,13},{1... | collective-permute-start | bytes 1572872 | tf_op jit(solution)/shard_map/ppermute | solution.py:79
  548.5 31.7 %collective-permute-start.31 = (bf16[512,512]{1,0:T(8,128)(2,1)S(1)}, bf16[512,512]{1,0:T(8,128)(2,1)S(1)}, u32[]{:S(2)}, u32[]{:S(2)}) collective-permute-start(bf16[512,512]{1,0:T(8,128)(2,1)S(1)} %add_convert_fusion.69), channel_id=1, source_target_pairs={{0,12},{1,13},{2,14},{3,15},{4,0},{5,1},{6,2},{7,3},{8,4},{9,5},{1... | collective-permute-start | bytes 1572872 | tf_op jit(solution)/shard_map/ppermute | solution.py:78
  552.8 28.3 %collective-permute-start.32 = (bf16[512,512]{1,0:T(8,128)(2,1)S(1)}, bf16[512,512]{1,0:T(8,128)(2,1)S(1)}, u32[]{:S(2)}, u32[]{:S(2)}) collective-permute-start(bf16[512,512]{1,0:T(8,128)(2,1)S(1)} %add_convert_fusion.69), channel_id=1, source_target_pairs={{0,4},{1,5},{2,6},{3,7},{4,8},{5,9},{6,10},{7,11},{8,12},{9,13},{1... | collective-permute-start | bytes 1572872 | tf_op jit(solution)/shard_map/ppermute | solution.py:79
  615.2 31.8 %collective-permute-start.35 = (bf16[512,512]{1,0:T(8,128)(2,1)S(1)}, bf16[512,512]{1,0:T(8,128)(2,1)S(1)}, u32[]{:S(2)}, u32[]{:S(2)}) collective-permute-start(bf16[512,512]{1,0:T(8,128)(2,1)S(1)} %add_convert_fusion.68), channel_id=1, source_target_pairs={{0,12},{1,13},{2,14},{3,15},{4,0},{5,1},{6,2},{7,3},{8,4},{9,5},{1... | collective-permute-start | bytes 1572872 | tf_op jit(solution)/shard_map/ppermute | solution.py:78
  619.6 28.3 %collective-permute-start.36 = (bf16[512,512]{1,0:T(8,128)(2,1)S(1)}, bf16[512,512]{1,0:T(8,128)(2,1)S(1)}, u32[]{:S(2)}, u32[]{:S(2)}) collective-permute-start(bf16[512,512]{1,0:T(8,128)(2,1)S(1)} %add_convert_fusion.68), channel_id=1, source_target_pairs={{0,4},{1,5},{2,6},{3,7},{4,8},{5,9},{6,10},{7,11},{8,12},{9,13},{1... | collective-permute-start | bytes 1572872 | tf_op jit(solution)/shard_map/ppermute | solution.py:79
  682.1 32.1 %collective-permute-start.39 = (bf16[512,512]{1,0:T(8,128)(2,1)S(1)}, bf16[512,512]{1,0:T(8,128)(2,1)S(1)}, u32[]{:S(2)}, u32[]{:S(2)}) collective-permute-start(bf16[512,512]{1,0:T(8,128)(2,1)S(1)} %add_convert_fusion.67), channel_id=1, source_target_pairs={{0,12},{1,13},{2,14},{3,15},{4,0},{5,1},{6,2},{7,3},{8,4},{9,5},{1... | collective-permute-start | bytes 1572872 | tf_op jit(solution)/shard_map/ppermute | solution.py:78
  686.4 28.5 %collective-permute-start.40 = (bf16[512,512]{1,0:T(8,128)(2,1)S(1)}, bf16[512,512]{1,0:T(8,128)(2,1)S(1)}, u32[]{:S(2)}, u32[]{:S(2)}) collective-permute-start(bf16[512,512]{1,0:T(8,128)(2,1)S(1)} %add_convert_fusion.67), channel_id=1, source_target_pairs={{0,4},{1,5},{2,6},{3,7},{4,8},{5,9},{6,10},{7,11},{8,12},{9,13},{1... | collective-permute-start | bytes 1572872 | tf_op jit(solution)/shard_map/ppermute | solution.py:79
  749.1 31.8 %collective-permute-start.43 = (bf16[512,512]{1,0:T(8,128)(2,1)S(1)}, bf16[512,512]{1,0:T(8,128)(2,1)S(1)}, u32[]{:S(2)}, u32[]{:S(2)}) collective-permute-start(bf16[512,512]{1,0:T(8,128)(2,1)S(1)} %add_convert_fusion.66), channel_id=1, source_target_pairs={{0,12},{1,13},{2,14},{3,15},{4,0},{5,1},{6,2},{7,3},{8,4},{9,5},{1... | collective-permute-start | bytes 1572872 | tf_op jit(solution)/shard_map/ppermute | solution.py:78
  753.4 28.3 %collective-permute-start.44 = (bf16[512,512]{1,0:T(8,128)(2,1)S(1)}, bf16[512,512]{1,0:T(8,128)(2,1)S(1)}, u32[]{:S(2)}, u32[]{:S(2)}) collective-permute-start(bf16[512,512]{1,0:T(8,128)(2,1)S(1)} %add_convert_fusion.66), channel_id=1, source_target_pairs={{0,4},{1,5},{2,6},{3,7},{4,8},{5,9},{6,10},{7,11},{8,12},{9,13},{1... | collective-permute-start | bytes 1572872 | tf_op jit(solution)/shard_map/ppermute | solution.py:79
  816.0 31.8 %collective-permute-start.47 = (bf16[512,512]{1,0:T(8,128)(2,1)S(1)}, bf16[512,512]{1,0:T(8,128)(2,1)S(1)}, u32[]{:S(2)}, u32[]{:S(2)}) collective-permute-start(bf16[512,512]{1,0:T(8,128)(2,1)S(1)} %add_convert_fusion.65), channel_id=1, source_target_pairs={{0,12},{1,13},{2,14},{3,15},{4,0},{5,1},{6,2},{7,3},{8,4},{9,5},{1... | collective-permute-start | bytes 1572872 | tf_op jit(solution)/shard_map/ppermute | solution.py:78
  820.3 28.3 %collective-permute-start.48 = (bf16[512,512]{1,0:T(8,128)(2,1)S(1)}, bf16[512,512]{1,0:T(8,128)(2,1)S(1)}, u32[]{:S(2)}, u32[]{:S(2)}) collective-permute-start(bf16[512,512]{1,0:T(8,128)(2,1)S(1)} %add_convert_fusion.65), channel_id=1, source_target_pairs={{0,4},{1,5},{2,6},{3,7},{4,8},{5,9},{6,10},{7,11},{8,12},{9,13},{1... | collective-permute-start | bytes 1572872 | tf_op jit(solution)/shard_map/ppermute | solution.py:79
  882.8 32.1 %collective-permute-start.51 = (bf16[512,512]{1,0:T(8,128)(2,1)S(1)}, bf16[512,512]{1,0:T(8,128)(2,1)S(1)}, u32[]{:S(2)}, u32[]{:S(2)}) collective-permute-start(bf16[512,512]{1,0:T(8,128)(2,1)S(1)} %add_convert_fusion.64), channel_id=1, source_target_pairs={{0,12},{1,13},{2,14},{3,15},{4,0},{5,1},{6,2},{7,3},{8,4},{9,5},{1... | collective-permute-start | bytes 1572872 | tf_op jit(solution)/shard_map/ppermute | solution.py:78
  887.1 28.6 %collective-permute-start.52 = (bf16[512,512]{1,0:T(8,128)(2,1)S(1)}, bf16[512,512]{1,0:T(8,128)(2,1)S(1)}, u32[]{:S(2)}, u32[]{:S(2)}) collective-permute-start(bf16[512,512]{1,0:T(8,128)(2,1)S(1)} %add_convert_fusion.64), channel_id=1, source_target_pairs={{0,4},{1,5},{2,6},{3,7},{4,8},{5,9},{6,10},{7,11},{8,12},{9,13},{1... | collective-permute-start | bytes 1572872 | tf_op jit(solution)/shard_map/ppermute | solution.py:79
  949.9 31.8 %collective-permute-start.55 = (bf16[512,512]{1,0:T(8,128)(2,1)S(1)}, bf16[512,512]{1,0:T(8,128)(2,1)S(1)}, u32[]{:S(2)}, u32[]{:S(2)}) collective-permute-start(bf16[512,512]{1,0:T(8,128)(2,1)S(1)} %add_convert_fusion.63), channel_id=1, source_target_pairs={{0,12},{1,13},{2,14},{3,15},{4,0},{5,1},{6,2},{7,3},{8,4},{9,5},{1... | collective-permute-start | bytes 1572872 | tf_op jit(solution)/shard_map/ppermute | solution.py:78
  954.2 28.3 %collective-permute-start.56 = (bf16[512,512]{1,0:T(8,128)(2,1)S(1)}, bf16[512,512]{1,0:T(8,128)(2,1)S(1)}, u32[]{:S(2)}, u32[]{:S(2)}) collective-permute-start(bf16[512,512]{1,0:T(8,128)(2,1)S(1)} %add_convert_fusion.63), channel_id=1, source_target_pairs={{0,4},{1,5},{2,6},{3,7},{4,8},{5,9},{6,10},{7,11},{8,12},{9,13},{1... | collective-permute-start | bytes 1572872 | tf_op jit(solution)/shard_map/ppermute | solution.py:79
  1016.8 31.8 %collective-permute-start.59 = (bf16[512,512]{1,0:T(8,128)(2,1)S(1)}, bf16[512,512]{1,0:T(8,128)(2,1)S(1)}, u32[]{:S(2)}, u32[]{:S(2)}) collective-permute-start(bf16[512,512]{1,0:T(8,128)(2,1)S(1)} %add_convert_fusion.62), channel_id=1, source_target_pairs={{0,12},{1,13},{2,14},{3,15},{4,0},{5,1},{6,2},{7,3},{8,4},{9,5},{1... | collective-permute-start | bytes 1572872 | tf_op jit(solution)/shard_map/ppermute | solution.py:78
  1021.1 28.4 %collective-permute-start.60 = (bf16[512,512]{1,0:T(8,128)(2,1)S(1)}, bf16[512,512]{1,0:T(8,128)(2,1)S(1)}, u32[]{:S(2)}, u32[]{:S(2)}) collective-permute-start(bf16[512,512]{1,0:T(8,128)(2,1)S(1)} %add_convert_fusion.62), channel_id=1, source_target_pairs={{0,4},{1,5},{2,6},{3,7},{4,8},{5,9},{6,10},{7,11},{8,12},{9,13},{1... | collective-permute-start | bytes 1572872 | tf_op jit(solution)/shard_map/ppermute | solution.py:79
  1083.7 32.0 %collective-permute-start.63 = (bf16[512,512]{1,0:T(8,128)(2,1)S(1)}, bf16[512,512]{1,0:T(8,128)(2,1)S(1)}, u32[]{:S(2)}, u32[]{:S(2)}) collective-permute-start(bf16[512,512]{1,0:T(8,128)(2,1)S(1)} %add_convert_fusion.61), channel_id=1, source_target_pairs={{0,12},{1,13},{2,14},{3,15},{4,0},{5,1},{6,2},{7,3},{8,4},{9,5},{1... | collective-permute-start | bytes 1572872 | tf_op jit(solution)/shard_map/ppermute | solution.py:78
  1088.0 28.6 %collective-permute-start.64 = (bf16[512,512]{1,0:T(8,128)(2,1)S(1)}, bf16[512,512]{1,0:T(8,128)(2,1)S(1)}, u32[]{:S(2)}, u32[]{:S(2)}) collective-permute-start(bf16[512,512]{1,0:T(8,128)(2,1)S(1)} %add_convert_fusion.61), channel_id=1, source_target_pairs={{0,4},{1,5},{2,6},{3,7},{4,8},{5,9},{6,10},{7,11},{8,12},{9,13},{1... | collective-permute-start | bytes 1572872 | tf_op jit(solution)/shard_map/ppermute | solution.py:79
  1221.6 29.5 %collective-permute-start.69 = (bf16[512,512]{1,0:T(8,128)(2,1)S(1)}, bf16[512,512]{1,0:T(8,128)(2,1)S(1)}, u32[]{:S(2)}, u32[]{:S(2)}) collective-permute-start(bf16[512,512]{1,0:T(8,128)(2,1)S(1)} %fusion.114), channel_id=1, source_target_pairs={{0,12},{1,13},{2,14},{3,15},{4,0},{5,1},{6,2},{7,3},{8,4},{9,5},{1... | collective-permute-start | bytes 1572872 | tf_op jit(solution)/shard_map/ppermute | solution.py:78
  1273.6 30.8 %collective-permute-start.73 = (bf16[512,512]{1,0:T(8,128)(2,1)S(1)}, bf16[512,512]{1,0:T(8,128)(2,1)S(1)}, u32[]{:S(2)}, u32[]{:S(2)}) collective-permute-start(bf16[512,512]{1,0:T(8,128)(2,1)S(1)} %add_convert_fusion.59), channel_id=1, source_target_pairs={{0,12},{1,13},{2,14},{3,15},{4,0},{5,1},{6,2},{7,3},{8,4},{9,5},{1... | collective-permute-start | bytes 1572872 | tf_op jit(solution)/shard_map/ppermute | solution.py:78
  1276.9 28.4 %collective-permute-start.74 = (bf16[512,512]{1,0:T(8,128)(2,1)S(1)}, bf16[512,512]{1,0:T(8,128)(2,1)S(1)}, u32[]{:S(2)}, u32[]{:S(2)}) collective-permute-start(bf16[512,512]{1,0:T(8,128)(2,1)S(1)} %add_convert_fusion.59), channel_id=1, source_target_pairs={{0,4},{1,5},{2,6},{3,7},{4,8},{5,9},{6,10},{7,11},{8,12},{9,13},{1... | collective-permute-start | bytes 1572872 | tf_op jit(solution)/shard_map/ppermute | solution.py:79
  1339.3 32.3 %collective-permute-start.77 = (bf16[512,512]{1,0:T(8,128)(2,1)S(1)}, bf16[512,512]{1,0:T(8,128)(2,1)S(1)}, u32[]{:S(2)}, u32[]{:S(2)}) collective-permute-start(bf16[512,512]{1,0:T(8,128)(2,1)S(1)} %add_convert_fusion.58), channel_id=1, source_target_pairs={{0,12},{1,13},{2,14},{3,15},{4,0},{5,1},{6,2},{7,3},{8,4},{9,5},{1... | collective-permute-start | bytes 1572872 | tf_op jit(solution)/shard_map/ppermute | solution.py:78
  1344.2 28.3 %collective-permute-start.78 = (bf16[512,512]{1,0:T(8,128)(2,1)S(1)}, bf16[512,512]{1,0:T(8,128)(2,1)S(1)}, u32[]{:S(2)}, u32[]{:S(2)}) collective-permute-start(bf16[512,512]{1,0:T(8,128)(2,1)S(1)} %add_convert_fusion.58), channel_id=1, source_target_pairs={{0,4},{1,5},{2,6},{3,7},{4,8},{5,9},{6,10},{7,11},{8,12},{9,13},{1... | collective-permute-start | bytes 1572872 | tf_op jit(solution)/shard_map/ppermute | solution.py:79
  1406.6 32.1 %collective-permute-start.81 = (bf16[512,512]{1,0:T(8,128)(2,1)S(1)}, bf16[512,512]{1,0:T(8,128)(2,1)S(1)}, u32[]{:S(2)}, u32[]{:S(2)}) collective-permute-start(bf16[512,512]{1,0:T(8,128)(2,1)S(1)} %add_convert_fusion.57), channel_id=1, source_target_pairs={{0,12},{1,13},{2,14},{3,15},{4,0},{5,1},{6,2},{7,3},{8,4},{9,5},{1... | collective-permute-start | bytes 1572872 | tf_op jit(solution)/shard_map/ppermute | solution.py:78
  1411.0 28.6 %collective-permute-start.82 = (bf16[512,512]{1,0:T(8,128)(2,1)S(1)}, bf16[512,512]{1,0:T(8,128)(2,1)S(1)}, u32[]{:S(2)}, u32[]{:S(2)}) collective-permute-start(bf16[512,512]{1,0:T(8,128)(2,1)S(1)} %add_convert_fusion.57), channel_id=1, source_target_pairs={{0,4},{1,5},{2,6},{3,7},{4,8},{5,9},{6,10},{7,11},{8,12},{9,13},{1... | collective-permute-start | bytes 1572872 | tf_op jit(solution)/shard_map/ppermute | solution.py:79
  1473.7 32.0 %collective-permute-start.85 = (bf16[512,512]{1,0:T(8,128)(2,1)S(1)}, bf16[512,512]{1,0:T(8,128)(2,1)S(1)}, u32[]{:S(2)}, u32[]{:S(2)}) collective-permute-start(bf16[512,512]{1,0:T(8,128)(2,1)S(1)} %add_convert_fusion.56), channel_id=1, source_target_pairs={{0,12},{1,13},{2,14},{3,15},{4,0},{5,1},{6,2},{7,3},{8,4},{9,5},{1... | collective-permute-start | bytes 1572872 | tf_op jit(solution)/shard_map/ppermute | solution.py:78
  1477.9 28.6 %collective-permute-start.86 = (bf16[512,512]{1,0:T(8,128)(2,1)S(1)}, bf16[512,512]{1,0:T(8,128)(2,1)S(1)}, u32[]{:S(2)}, u32[]{:S(2)}) collective-permute-start(bf16[512,512]{1,0:T(8,128)(2,1)S(1)} %add_convert_fusion.56), channel_id=1, source_target_pairs={{0,4},{1,5},{2,6},{3,7},{4,8},{5,9},{6,10},{7,11},{8,12},{9,13},{1... | collective-permute-start | bytes 1572872 | tf_op jit(solution)/shard_map/ppermute | solution.py:79
  1540.6 31.9 %collective-permute-start.89 = (bf16[512,512]{1,0:T(8,128)(2,1)S(1)}, bf16[512,512]{1,0:T(8,128)(2,1)S(1)}, u32[]{:S(2)}, u32[]{:S(2)}) collective-permute-start(bf16[512,512]{1,0:T(8,128)(2,1)S(1)} %add_convert_fusion.55), channel_id=1, source_target_pairs={{0,12},{1,13},{2,14},{3,15},{4,0},{5,1},{6,2},{7,3},{8,4},{9,5},{1... | collective-permute-start | bytes 1572872 | tf_op jit(solution)/shard_map/ppermute | solution.py:78
  1545.0 28.4 %collective-permute-start.90 = (bf16[512,512]{1,0:T(8,128)(2,1)S(1)}, bf16[512,512]{1,0:T(8,128)(2,1)S(1)}, u32[]{:S(2)}, u32[]{:S(2)}) collective-permute-start(bf16[512,512]{1,0:T(8,128)(2,1)S(1)} %add_convert_fusion.55), channel_id=1, source_target_pairs={{0,4},{1,5},{2,6},{3,7},{4,8},{5,9},{6,10},{7,11},{8,12},{9,13},{1... | collective-permute-start | bytes 1572872 | tf_op jit(solution)/shard_map/ppermute | solution.py:79
  1607.4 31.7 %collective-permute-start.93 = (bf16[512,512]{1,0:T(8,128)(2,1)S(1)}, bf16[512,512]{1,0:T(8,128)(2,1)S(1)}, u32[]{:S(2)}, u32[]{:S(2)}) collective-permute-start(bf16[512,512]{1,0:T(8,128)(2,1)S(1)} %add_convert_fusion.54), channel_id=1, source_target_pairs={{0,12},{1,13},{2,14},{3,15},{4,0},{5,1},{6,2},{7,3},{8,4},{9,5},{1... | collective-permute-start | bytes 1572872 | tf_op jit(solution)/shard_map/ppermute | solution.py:78
  1611.6 28.4 %collective-permute-start.94 = (bf16[512,512]{1,0:T(8,128)(2,1)S(1)}, bf16[512,512]{1,0:T(8,128)(2,1)S(1)}, u32[]{:S(2)}, u32[]{:S(2)}) collective-permute-start(bf16[512,512]{1,0:T(8,128)(2,1)S(1)} %add_convert_fusion.54), channel_id=1, source_target_pairs={{0,4},{1,5},{2,6},{3,7},{4,8},{5,9},{6,10},{7,11},{8,12},{9,13},{1... | collective-permute-start | bytes 1572872 | tf_op jit(solution)/shard_map/ppermute | solution.py:79
  1674.1 32.0 %collective-permute-start.97 = (bf16[512,512]{1,0:T(8,128)(2,1)S(1)}, bf16[512,512]{1,0:T(8,128)(2,1)S(1)}, u32[]{:S(2)}, u32[]{:S(2)}) collective-permute-start(bf16[512,512]{1,0:T(8,128)(2,1)S(1)} %add_convert_fusion.53), channel_id=1, source_target_pairs={{0,12},{1,13},{2,14},{3,15},{4,0},{5,1},{6,2},{7,3},{8,4},{9,5},{1... | collective-permute-start | bytes 1572872 | tf_op jit(solution)/shard_map/ppermute | solution.py:78
  1678.3 28.6 %collective-permute-start.98 = (bf16[512,512]{1,0:T(8,128)(2,1)S(1)}, bf16[512,512]{1,0:T(8,128)(2,1)S(1)}, u32[]{:S(2)}, u32[]{:S(2)}) collective-permute-start(bf16[512,512]{1,0:T(8,128)(2,1)S(1)} %add_convert_fusion.53), channel_id=1, source_target_pairs={{0,4},{1,5},{2,6},{3,7},{4,8},{5,9},{6,10},{7,11},{8,12},{9,13},{1... | collective-permute-start | bytes 1572872 | tf_op jit(solution)/shard_map/ppermute | solution.py:79
  1741.0 31.7 %collective-permute-start.101 = (bf16[512,512]{1,0:T(8,128)(2,1)S(1)}, bf16[512,512]{1,0:T(8,128)(2,1)S(1)}, u32[]{:S(2)}, u32[]{:S(2)}) collective-permute-start(bf16[512,512]{1,0:T(8,128)(2,1)S(1)} %add_convert_fusion.52), channel_id=1, source_target_pairs={{0,12},{1,13},{2,14},{3,15},{4,0},{5,1},{6,2},{7,3},{8,4},{9,5},{1... | collective-permute-start | bytes 1572872 | tf_op jit(solution)/shard_map/ppermute | solution.py:78
  1745.2 28.3 %collective-permute-start.102 = (bf16[512,512]{1,0:T(8,128)(2,1)S(1)}, bf16[512,512]{1,0:T(8,128)(2,1)S(1)}, u32[]{:S(2)}, u32[]{:S(2)}) collective-permute-start(bf16[512,512]{1,0:T(8,128)(2,1)S(1)} %add_convert_fusion.52), channel_id=1, source_target_pairs={{0,4},{1,5},{2,6},{3,7},{4,8},{5,9},{6,10},{7,11},{8,12},{9,13},{1... | collective-permute-start | bytes 1572872 | tf_op jit(solution)/shard_map/ppermute | solution.py:79
  1807.6 31.8 %collective-permute-start.105 = (bf16[512,512]{1,0:T(8,128)(2,1)S(1)}, bf16[512,512]{1,0:T(8,128)(2,1)S(1)}, u32[]{:S(2)}, u32[]{:S(2)}) collective-permute-start(bf16[512,512]{1,0:T(8,128)(2,1)S(1)} %add_convert_fusion.51), channel_id=1, source_target_pairs={{0,12},{1,13},{2,14},{3,15},{4,0},{5,1},{6,2},{7,3},{8,4},{9,5},{1... | collective-permute-start | bytes 1572872 | tf_op jit(solution)/shard_map/ppermute | solution.py:78
  1811.9 28.4 %collective-permute-start.106 = (bf16[512,512]{1,0:T(8,128)(2,1)S(1)}, bf16[512,512]{1,0:T(8,128)(2,1)S(1)}, u32[]{:S(2)}, u32[]{:S(2)}) collective-permute-start(bf16[512,512]{1,0:T(8,128)(2,1)S(1)} %add_convert_fusion.51), channel_id=1, source_target_pairs={{0,4},{1,5},{2,6},{3,7},{4,8},{5,9},{6,10},{7,11},{8,12},{9,13},{1... | collective-permute-start | bytes 1572872 | tf_op jit(solution)/shard_map/ppermute | solution.py:79
  1874.4 31.9 %collective-permute-start.109 = (bf16[512,512]{1,0:T(8,128)(2,1)S(1)}, bf16[512,512]{1,0:T(8,128)(2,1)S(1)}, u32[]{:S(2)}, u32[]{:S(2)}) collective-permute-start(bf16[512,512]{1,0:T(8,128)(2,1)S(1)} %add_convert_fusion.50), channel_id=1, source_target_pairs={{0,12},{1,13},{2,14},{3,15},{4,0},{5,1},{6,2},{7,3},{8,4},{9,5},{1... | collective-permute-start | bytes 1572872 | tf_op jit(solution)/shard_map/ppermute | solution.py:78
  1878.6 28.5 %collective-permute-start.110 = (bf16[512,512]{1,0:T(8,128)(2,1)S(1)}, bf16[512,512]{1,0:T(8,128)(2,1)S(1)}, u32[]{:S(2)}, u32[]{:S(2)}) collective-permute-start(bf16[512,512]{1,0:T(8,128)(2,1)S(1)} %add_convert_fusion.50), channel_id=1, source_target_pairs={{0,4},{1,5},{2,6},{3,7},{4,8},{5,9},{6,10},{7,11},{8,12},{9,13},{1... | collective-permute-start | bytes 1572872 | tf_op jit(solution)/shard_map/ppermute | solution.py:79
  1941.2 31.8 %collective-permute-start.113 = (bf16[512,512]{1,0:T(8,128)(2,1)S(1)}, bf16[512,512]{1,0:T(8,128)(2,1)S(1)}, u32[]{:S(2)}, u32[]{:S(2)}) collective-permute-start(bf16[512,512]{1,0:T(8,128)(2,1)S(1)} %add_convert_fusion.49), channel_id=1, source_target_pairs={{0,12},{1,13},{2,14},{3,15},{4,0},{5,1},{6,2},{7,3},{8,4},{9,5},{1... | collective-permute-start | bytes 1572872 | tf_op jit(solution)/shard_map/ppermute | solution.py:78
  1945.5 28.3 %collective-permute-start.114 = (bf16[512,512]{1,0:T(8,128)(2,1)S(1)}, bf16[512,512]{1,0:T(8,128)(2,1)S(1)}, u32[]{:S(2)}, u32[]{:S(2)}) collective-permute-start(bf16[512,512]{1,0:T(8,128)(2,1)S(1)} %add_convert_fusion.49), channel_id=1, source_target_pairs={{0,4},{1,5},{2,6},{3,7},{4,8},{5,9},{6,10},{7,11},{8,12},{9,13},{1... | collective-permute-start | bytes 1572872 | tf_op jit(solution)/shard_map/ppermute | solution.py:79
  2007.9 31.7 %collective-permute-start.117 = (bf16[512,512]{1,0:T(8,128)(2,1)S(1)}, bf16[512,512]{1,0:T(8,128)(2,1)S(1)}, u32[]{:S(2)}, u32[]{:S(2)}) collective-permute-start(bf16[512,512]{1,0:T(8,128)(2,1)S(1)} %add_convert_fusion.48), channel_id=1, source_target_pairs={{0,12},{1,13},{2,14},{3,15},{4,0},{5,1},{6,2},{7,3},{8,4},{9,5},{1... | collective-permute-start | bytes 1572872 | tf_op jit(solution)/shard_map/ppermute | solution.py:78
  2012.2 28.3 %collective-permute-start.118 = (bf16[512,512]{1,0:T(8,128)(2,1)S(1)}, bf16[512,512]{1,0:T(8,128)(2,1)S(1)}, u32[]{:S(2)}, u32[]{:S(2)}) collective-permute-start(bf16[512,512]{1,0:T(8,128)(2,1)S(1)} %add_convert_fusion.48), channel_id=1, source_target_pairs={{0,4},{1,5},{2,6},{3,7},{4,8},{5,9},{6,10},{7,11},{8,12},{9,13},{1... | collective-permute-start | bytes 1572872 | tf_op jit(solution)/shard_map/ppermute | solution.py:79
  2074.6 32.0 %collective-permute-start.121 = (bf16[512,512]{1,0:T(8,128)(2,1)S(1)}, bf16[512,512]{1,0:T(8,128)(2,1)S(1)}, u32[]{:S(2)}, u32[]{:S(2)}) collective-permute-start(bf16[512,512]{1,0:T(8,128)(2,1)S(1)} %add_convert_fusion.47), channel_id=1, source_target_pairs={{0,12},{1,13},{2,14},{3,15},{4,0},{5,1},{6,2},{7,3},{8,4},{9,5},{1... | collective-permute-start | bytes 1572872 | tf_op jit(solution)/shard_map/ppermute | solution.py:78
  2078.9 28.6 %collective-permute-start.122 = (bf16[512,512]{1,0:T(8,128)(2,1)S(1)}, bf16[512,512]{1,0:T(8,128)(2,1)S(1)}, u32[]{:S(2)}, u32[]{:S(2)}) collective-permute-start(bf16[512,512]{1,0:T(8,128)(2,1)S(1)} %add_convert_fusion.47), channel_id=1, source_target_pairs={{0,4},{1,5},{2,6},{3,7},{4,8},{5,9},{6,10},{7,11},{8,12},{9,13},{1... | collective-permute-start | bytes 1572872 | tf_op jit(solution)/shard_map/ppermute | solution.py:79
  2141.6 31.7 %collective-permute-start.125 = (bf16[512,512]{1,0:T(8,128)(2,1)S(1)}, bf16[512,512]{1,0:T(8,128)(2,1)S(1)}, u32[]{:S(2)}, u32[]{:S(2)}) collective-permute-start(bf16[512,512]{1,0:T(8,128)(2,1)S(1)} %add_convert_fusion.46), channel_id=1, source_target_pairs={{0,12},{1,13},{2,14},{3,15},{4,0},{5,1},{6,2},{7,3},{8,4},{9,5},{1... | collective-permute-start | bytes 1572872 | tf_op jit(solution)/shard_map/ppermute | solution.py:78
  2145.8 28.3 %collective-permute-start.126 = (bf16[512,512]{1,0:T(8,128)(2,1)S(1)}, bf16[512,512]{1,0:T(8,128)(2,1)S(1)}, u32[]{:S(2)}, u32[]{:S(2)}) collective-permute-start(bf16[512,512]{1,0:T(8,128)(2,1)S(1)} %add_convert_fusion.46), channel_id=1, source_target_pairs={{0,4},{1,5},{2,6},{3,7},{4,8},{5,9},{6,10},{7,11},{8,12},{9,13},{1... | collective-permute-start | bytes 1572872 | tf_op jit(solution)/shard_map/ppermute | solution.py:79
  2208.2 31.8 %collective-permute-start.129 = (bf16[512,512]{1,0:T(8,128)(2,1)S(1)}, bf16[512,512]{1,0:T(8,128)(2,1)S(1)}, u32[]{:S(2)}, u32[]{:S(2)}) collective-permute-start(bf16[512,512]{1,0:T(8,128)(2,1)S(1)} %add_convert_fusion.45), channel_id=1, source_target_pairs={{0,12},{1,13},{2,14},{3,15},{4,0},{5,1},{6,2},{7,3},{8,4},{9,5},{1... | collective-permute-start | bytes 1572872 | tf_op jit(solution)/shard_map/ppermute | solution.py:78
  2212.5 28.4 %collective-permute-start.130 = (bf16[512,512]{1,0:T(8,128)(2,1)S(1)}, bf16[512,512]{1,0:T(8,128)(2,1)S(1)}, u32[]{:S(2)}, u32[]{:S(2)}) collective-permute-start(bf16[512,512]{1,0:T(8,128)(2,1)S(1)} %add_convert_fusion.45), channel_id=1, source_target_pairs={{0,4},{1,5},{2,6},{3,7},{4,8},{5,9},{6,10},{7,11},{8,12},{9,13},{1... | collective-permute-start | bytes 1572872 | tf_op jit(solution)/shard_map/ppermute | solution.py:79
  (159 other events, 3634.2 us)
where the time goes:
time: 2320 us; the launch traced here: 2310 us
  matrix products  745 us (32%)
  waiting for transfers between devices  563 us (24%)
  other arithmetic  366 us (16%)
  local copies, waits for them, and re-layouts  357 us (15%)
  starting transfers between devices  273 us (12%)
    dot_general x186, matrix products, matmul_f32(): return jnp.dot(values, weight, preferred_element_type=jnp.float32)  737 us
    ppermute x32, waiting for transfers between devices, local_run(): lax.ppermute(mesh_cur[mesh_dev - half_shard:], 'gp', shift_pairs(1))  558 us
    unnamed x471, local copies, waits for them, and re-layouts  275 us
    reduce_sum x32, other arithmetic, local_run(): edge_sum = jnp.sum(edge_lat, axis=1, dtype=jnp.float32).astype(jnp.bfloat16)  184 us
    reduce_sum x80, other arithmetic, layer_norm(): spread = jnp.mean(centred * centred, axis=-1, keepdims=True)  145 us
    ppermute x32, starting transfers between devices, local_run(): far_plus = lax.ppermute(mesh_cur, 'gp', shift_pairs(-quarter_hop))  135 us
    ppermute x32, starting transfers between devices, local_run(): lax.ppermute(mesh_cur[mesh_dev - half_shard:], 'gp', shift_pairs(1))  87.9 us
  transfers between devices with their start and end apart: 132, of which 37 were waited for; matrix products, arithmetic and copies ran while one was open for 12% of the time, Pallas kernels for 0%

commit v1 on v0

v1 whole, which is shorter than its diff:
```python
import functools

import jax
import jax.numpy as jnp
from jax import lax
from jax.experimental import pallas as pl
from jax.experimental.pallas import tpu as pltpu
from jax.sharding import PartitionSpec as P

F32 = jnp.float32
BF16 = jnp.bfloat16
SLAB = 16
RATIO = 2
OFFSETS = 6


def dot(a, b):
    return jnp.dot(a, b, preferred_element_type=F32)


def dot_t(a, b):
    return lax.dot_general(a, b, (((0,), (0,)), ((), ())), preferred_element_type=F32)


def dot_bt(a, b):
    return lax.dot_general(a, b, (((1,), (1,)), ((), ())), preferred_element_type=F32)


def silu(x):
    half = 0.5 * x
    return half * jnp.tanh(half) + half


def layer_norm(y):
    centred = y - jnp.mean(y, axis=-1, keepdims=True)
    spread = jnp.mean(centred * centred, axis=-1, keepdims=True)
    return centred * lax.rsqrt(spread + 1e-5)


def kernel(cfg, *refs):
    names = cfg["names"]
    r = dict(zip(names, refs, strict=True))
    n, rows, latent, shift, layers = cfg["n"], cfg["rows"], cfg["latent"], cfg["shift"], cfg["layers"]
    nvar, in_feat = cfg["nvar"], cfg["in_feat"]
    cols_j = n * rows // shift
    nblk = shift // n
    quarter = cols_j // 4
    grid_rows = RATIO * rows
    per_blk = OFFSETS * cols_j
    bpc = 2
    chunk = bpc * per_blk
    nchunk = nblk // bpc
    order = [(p + 1) % nblk for p in range(nblk)]
    me = lax.axis_index("gp")
    left = lax.rem(me + n - 1, n)
    right = lax.rem(me + 1, n)
    pre, hid, ys = (r["p0"], r["p1"]), (r["h0"], r["h1"]), (r["y0"], r["y1"])

    def remote(src, dst, send, recv, dev):
        return pltpu.make_async_remote_copy(src_ref=src, dst_ref=dst, send_sem=send, recv_sem=recv, device_id={"gp": dev}, device_id_type=pl.DeviceIdType.MESH)

    last = layers + 1
    loads = {
        "xp": (r["xp_h"], r["xs"].at[0]),
        "xc": (r["xc_h"], r["xs"].at[1]),
        "fs": (r["fs_h"], r["fs"]),
        "ns": (r["ns_h"], r["ns"]),
        "gm": (r["gm_h"], r["gm"]),
        "mf": (r["mf_h"], r["mf"]),
        "ew": (r["ew_h"], r["ew"]),
        "wg": (r["wg_h"], r["wg"].at[0:in_feat]),
        "wemb": (r["wemb_h"], r["wemb"]),
        "wi0": (r["wei_h"].at[0], r["wi"].at[0]),
        "wo0": (r["weo_h"].at[0], r["wo"].at[0]),
        "ni0": (r["wni_h"].at[0], r["ni"].at[0]),
        "no0": (r["wno_h"].at[0], r["no"].at[0]),
        "wself": (r["wself_h"], r["wself"]),
        "wi1": (r["wei_h"].at[last], r["wi"].at[1]),
        "wo1": (r["weo_h"].at[last], r["wo"].at[1]),
        "ni1": (r["wni_h"].at[last], r["ni"].at[1]),
        "no1": (r["wno_h"].at[last], r["no"].at[1]),
        "woh": (r["woh_h"], r["woh"]),
        "wof": (r["wof_h"], r["wof"]),
    }
    loads = {key: pltpu.make_async_copy(src, dst, r["load_sem"].at[i]) for i, (key, (src, dst)) in enumerate(loads.items())}

    def fetch(layer, slot):
        pairs = ((r["wei_h"], r["lwi"]), (r["weo_h"], r["lwo"]), (r["wni_h"], r["lni"]), (r["wno_h"], r["lno"]))
        return [pltpu.make_async_copy(src.at[layer], dst.at[slot], r["fetch_sem"].at[slot, i]) for i, (src, dst) in enumerate(pairs)]

    for key in ("gm", "mf", "ew", "xp", "xc", "fs", "ns", "wg", "wemb", "wi0", "wo0", "ni0", "no0", "wself", "wi1", "wo1", "ni1", "no1", "woh", "wof"):
        loads[key].start()
    for c in fetch(1, 0):
        c.start()

    barrier = pltpu.get_barrier_semaphore()
    for off in range(1, n):
        pl.semaphore_signal(barrier, inc=1, device_id={"gp": lax.rem(me + off, n)}, device_id_type=pl.DeviceIdType.MESH)

    def iota(shape, dim):
        return lax.broadcasted_iota(jnp.int32, shape, dim)

    def onehot(pred):
        return jnp.where(pred, 1.0, 0.0).astype(BF16)

    def perm(shape, slot_dim):
        slot, row = iota(shape, slot_dim), iota(shape, 1 - slot_dim)
        jp = lax.rem(lax.rem(row, cols_j) + (cols_j - 1), cols_j)
        return onehot(slot == jp * nblk + lax.div(row, cols_j))

    for t in range(rows // 128):
        sl = slice(128 * t, 128 * t + 128)
        slot, row = iota((128, rows), 1), iota((128, rows), 0) + 128 * t
        jp = lax.rem(lax.rem(row, cols_j) + (cols_j - 1), cols_j)
        r["pfwd"][sl, :] = onehot(slot == jp * nblk + lax.div(row, cols_j))
        slot, row = iota((128, rows), 0) + 128 * t, iota((128, rows), 1)
        jp = lax.rem(lax.rem(row, cols_j) + (cols_j - 1), cols_j)
        r["pbwd"][sl, :] = onehot(slot == jp * nblk + lax.div(row, cols_j))
    half = rows // 2
    r["ex"][...] = onehot(lax.div(iota((rows, half), 0), RATIO) == iota((rows, half), 1))
    r["ps"][...] = onehot(iota((half, rows), 0) == lax.div(iota((half, rows), 1), RATIO))
    r["wg"][in_feat:, :] = jnp.zeros((r["wg"].shape[0] - in_feat, latent), BF16)

    def act(p, count, hidden, add=None):
        for o in range(0, count, SLAB):
            x = p[o:o + SLAB, :]
            if add is not None:
                x = x + add(o)
            hidden[o:o + SLAB, :] = silu(x).astype(BF16)

    def finish(y, count, store):
        for o in range(0, count, SLAB):
            store(o, layer_norm(y[o:o + SLAB, :]))

    loads["gm"].wait()
    loads["mf"].wait()
    loads["ew"].wait()
    eye = onehot(iota((32, 128), 0) == iota((32, 128), 1))
    r["feat"][...] = dot_t(r["mf"][0:32, :], eye).astype(BF16).reshape(2, half, 128)
    pl.semaphore_wait(barrier, n - 1)

    def feat_copy(off, jj, dev, owner):
        slot = lax.rem(2 * owner + jj + cols_j - 1, cols_j)
        return remote(r["feat"].at[jj, pl.ds(pl.multiple_of(nblk * dev, nblk), nblk), :], r["fin"].at[slot], r["fsend"].at[off, jj], r["frecv"].at[off, jj], dev)

    nb_copies = [
        remote(r["mf"].at[32:48, 0:half], r["mfp"].at[:, half:], r["nsend"].at[0], r["nrecv"].at[0], left),
        remote(r["gm"].at[0, :, 0:rows], r["g2p"].at[:, rows:], r["nsend"].at[1], r["nrecv"].at[1], left),
    ]
    for c in nb_copies:
        c.start()
    for off in range(1, n):
        for jj in range(2):
            feat_copy(off, jj, lax.rem(me + off, n), me).start()
    for jj in range(2):
        r["fin"][lax.rem(2 * me + jj + cols_j - 1, cols_j)] = r["feat"][jj, pl.ds(pl.multiple_of(nblk * me, nblk), nblk), :]
    r["mfp"][:, 0:half] = r["mf"][32:48, half:]
    r["g2p"][:, 0:rows] = r["gm"][0, :, rows:]

    loads["wemb"].wait()

    def embed(lhs_t, w_first, w_second, store):
        pre[0][0:rows, :] = dot_t(lhs_t, w_first)
        act(pre[0], rows, hid[0])
        ys[0][0:rows, :] = dot(hid[0][0:rows, :], w_second)
        finish(ys[0], rows, store)

    loads["wi1"].wait()

    def m2g_body(q, _):
        base = pl.multiple_of(q * rows, rows)

        def store(o, v):
            r["m2g"][pl.ds(base + o, SLAB), :] = v.astype(BF16)

        embed(r["gm"][1, :, pl.ds(base, rows)], r["ew"][2], r["wemb"][3], store)
        r["decst"][pl.ds(base, rows), :] = dot(r["m2g"][pl.ds(base, rows), :], r["wi"][1, 0:latent, :])
        return 0

    lax.fori_loop(0, RATIO, m2g_body, 0)

    for c in nb_copies:
        c.wait()
    loads["wi0"].wait()
    loads["ni0"].wait()

    def store_mesh(o, v):
        r["mlat"][o:o + SLAB, :] = v.astype(BF16)

    embed(r["mfp"][...], r["ew"][0], r["wemb"][1], store_mesh)
    r["nodst"][...] = dot(r["mlat"][...], r["ni"][0, 0:latent, :])

    def g2m_body(q, _):
        base = pl.multiple_of(q * rows, rows)
        hbase = pl.multiple_of(q * half, half)

        def store(o, v):
            r["g2m"][pl.ds(base + o, SLAB), :] = v.astype(BF16)

        embed(r["g2p"][:, pl.ds(base, rows)], r["ew"][1], r["wemb"][2], store)
        hid[1][0:rows, :] = dot(r["ex"][...], r["mlat"][pl.ds(hbase, half), :]).astype(BF16)
        r["encst"][pl.ds(base, rows), :] = dot(r["g2m"][pl.ds(base, rows), :], r["wi"][0, 0:latent, :]) + dot(hid[1][0:rows, :], r["wi"][0, 2 * latent:, :])
        return 0

    lax.fori_loop(0, RATIO, g2m_body, 0)

    for off in range(1, n):
        for jj in range(2):
            feat_copy(off, jj, lax.rem(me + off, n), lax.rem(me + n - off, n)).wait()
    r["featm"][...] = dot(r["pfwd"][...], r["fin"][...].reshape(rows, 128)).astype(BF16)

    def edge_body(k, _):
        sel = onehot(iota((128, 16), 0) == iota((128, 16), 1) + 4 * k)
        sel = jnp.where(iota((128, 16), 1) < 4, sel, jnp.zeros_like(sel))
        w_k = dot(sel, r["ew"][3]).astype(BF16)
        pre[0][0:rows, :] = dot(r["featm"][...], w_k)
        act(pre[0], rows, hid[0])
        ys[0][0:rows, :] = dot(hid[0][0:rows, :], r["wemb"][4])

        def store(o, v):
            pos = order.index(o // cols_j)
            at = pl.multiple_of(pos * per_blk + k * cols_j + o % cols_j, SLAB)
            r["ebase"][pl.ds(at, SLAB), :] = v.astype(BF16)

        finish(ys[0], rows, store)
        return 0

    lax.fori_loop(0, OFFSETS, edge_body, 0)

    for key in ("xp", "xc", "fs", "ns", "wg", "wo0", "no0", "wself", "wo1", "ni1", "no1", "woh", "wof"):
        loads[key].wait()

    def to_blocks(off, dev, owner):
        return remote(r["mcur"].at[:, pl.ds(pl.multiple_of(nblk * dev, nblk), nblk), :], r["hin"].at[pl.ds(2 * owner, 2)], r["asend"].at[off], r["arecv"].at[off], dev)

    def to_grid(off, dev, owner):
        return remote(r["yout"].at[pl.ds(2 * dev, 2)], r["hb"].at[:, pl.ds(pl.multiple_of(nblk * owner, nblk), nblk), :], r["bsend"].at[off], r["brecv"].at[off], dev)

    def layer_body(it, slot0):
        slot = lax.rem(it + slot0, 2)
        par = slot
        for c in fetch(it + 1, slot):
            c.wait()
        for c in fetch(jnp.where(it + 1 < layers, it + 2, 1), 1 - slot):
            c.start()
        wi, wo, ni, no = r["lwi"].at[slot], r["lwo"].at[slot], r["lni"].at[slot], r["lno"].at[slot]
        s0, sup, sdn, rr, n1, e, h = r["s0"], r["sup"], r["sdn"], r["rr"], r["n1"], r["e"], r["h"]
        hv = h[...]
        s0[cols_j:cols_j + rows, :] = dot(hv, wi[latent:2 * latent, :])
        rr[...] = dot(hv, wi[2 * latent:, :])
        n1[...] = dot(hv, ni[0:latent, :])
        for b in range(nblk):
            blk = s0[(b + 1) * cols_j:(b + 2) * cols_j, :]
            sup[b * cols_j:(b + 1) * cols_j, :] = jnp.concatenate([blk[1:], blk[:1]], axis=0)
            sdn[b * cols_j:(b + 1) * cols_j, :] = jnp.concatenate([blk[-1:], blk[:-1]], axis=0)
        halo = [
            remote(s0.at[nblk * cols_j:(nblk + 1) * cols_j], r["halo"].at[par, 0], r["hsend"].at[0], r["hrecv"].at[par, 0], right),
            remote(s0.at[cols_j:2 * cols_j], r["halo"].at[par, 1], r["hsend"].at[1], r["hrecv"].at[par, 1], left),
        ]
        for c in halo:
            c.start()

        def send(b, k, g):
            at = SLAB * g
            if k == 0:
                return s0[(b + 2) * cols_j + at:(b + 2) * cols_j + at + SLAB, :]
            if k == 1:
                return s0[b * cols_j + at:b * cols_j + at + SLAB, :]
            if k == 2:
                return sup[b * cols_j + at:b * cols_j + at + SLAB, :]
            if k == 3:
                return sdn[b * cols_j + at:b * cols_j + at + SLAB, :]
            sh = quarter if k == 4 else -quarter
            base = (b + 1) * cols_j
            lo, hi = (at + sh) % cols_j, (at + 8 + sh) % cols_j
            return jnp.concatenate([s0[base + lo:base + lo + 8, :], s0[base + hi:base + hi + 8, :]], axis=0)

        def edge_act(i):
            for bb in range(bpc):
                b = order[i * bpc + bb]
                for g in range(cols_j // SLAB):
                    recv = rr[b * cols_j + SLAB * g:b * cols_j + SLAB * g + SLAB, :]
                    for k in range(OFFSETS):
                        o = (bb * OFFSETS + k) * cols_j + SLAB * g
                        hid[i % 2][o:o + SLAB, :] = silu(pre[i % 2][o:o + SLAB, :] + send(b, k, g) + recv).astype(BF16)

        def edge_finish(i):
            y = ys[i % 2]
            for bb in range(bpc):
                b = order[i * bpc + bb]
                for g in range(cols_j // SLAB):
                    total = None
                    for k in range(OFFSETS):
                        o = (bb * OFFSETS + k) * cols_j + SLAB * g
                        eo = i * chunk + o
                        new = (e[eo:eo + SLAB, :].astype(F32) + layer_norm(y[o:o + SLAB, :])).astype(BF16)
                        e[eo:eo + SLAB, :] = new
                        total = new.astype(F32) if total is None else total + new.astype(F32)
                    r["esum"][b * cols_j + SLAB * g:b * cols_j + SLAB * g + SLAB, :] = total.astype(BF16)

        for i in range(nchunk + 2):
            if i < nchunk:
                pre[i % 2][0:chunk, :] = dot(e[i * chunk:(i + 1) * chunk, :], wi[0:latent, :])
            if i == nchunk:
                for c in halo:
                    c.wait()
                low, high = r["halo"][par, 0], r["halo"][par, 1]
                low_w = jnp.concatenate([low[-1:], low[:-1]], axis=0)
                high_w = jnp.concatenate([high[1:], high[:1]], axis=0)
                s0[0:cols_j, :] = jnp.where(me == 0, low_w, low)
                s0[(nblk + 1) * cols_j:, :] = jnp.where(me == n - 1, high_w, high)
            if 1 <= i < nchunk + 1:
                edge_act(i - 1)
                ys[(i - 1) % 2][0:chunk, :] = dot(hid[(i - 1) % 2][0:chunk, :], wo[...])
            if i >= 2:
                edge_finish(i - 2)
        for q in range(2):
            base = q * half
            pre[q][0:half, :] = dot(r["esum"][base:base + half, :], ni[latent:, :])
            act(pre[q], half, hid[q], lambda o, base=base: n1[base + o:base + o + SLAB, :])
            ys[q][0:half, :] = dot(hid[q][0:half, :], no[...])

            def store(o, v, base=base):
                at = slice(base + o, base + o + SLAB)
                h[at, :] = (h[at, :].astype(F32) + v).astype(BF16)

            finish(ys[q], half, store)
        return slot0

    def step_body(s, _):
        x_prev, x_cur = r["xs"].at[s], r["xs"].at[1 - s]
        mean, std, dmean, dstd = (r["ns"][:, i:i + 1] for i in range(4))

        def grid_body(q, _):
            base = pl.multiple_of(q * rows, rows)
            at = pl.ds(base, rows)
            p = pre[0]
            p[0:nvar, :] = (x_prev[:, at] - mean) / std
            p[nvar:2 * nvar, :] = (x_cur[:, at] - mean) / std
            p[2 * nvar:in_feat, :] = r["fs"][s, :, at]
            p[in_feat:, :] = jnp.zeros((p.shape[0] - in_feat, rows), F32)
            hid[0][...] = p[...].astype(BF16)
            pre[1][...] = dot_t(hid[0][...], r["wg"][...])
            act(pre[1], rows, hid[1])
            ys[1][...] = dot(hid[1][...], r["wemb"][0])

            def store(o, v):
                r["gl"][pl.ds(base + o, SLAB), :] = v.astype(BF16)

            finish(ys[1], rows, store)
            pre[0][...] = dot(r["gl"][at, :], r["wi"][0, latent:2 * latent, :])
            act(pre[0], rows, hid[0], lambda o: r["encst"][pl.ds(base + o, SLAB), :])
            ys[0][...] = dot(hid[0][...], r["wo"][0])

            def store_edge(o, v):
                hid[1][o:o + SLAB, :] = (r["g2m"][pl.ds(base + o, SLAB), :].astype(F32) + v).astype(BF16)

            finish(ys[0], rows, store_edge)
            hbase = pl.multiple_of(q * half, half)
            esum = dot(r["ps"][...], hid[1][...]).astype(BF16)
            pre[1][0:half, :] = dot(esum, r["ni"][0, latent:, :])
            act(pre[1], half, hid[0], lambda o: r["nodst"][pl.ds(hbase + o, SLAB), :])
            ys[1][0:half, :] = dot(hid[0][0:half, :], r["no"][0])

            def store_node(o, v):
                r["mcur"][q, o:o + SLAB, :] = (r["mlat"][pl.ds(hbase + o, SLAB), :].astype(F32) + v).astype(BF16)

            finish(ys[1], half, store_node)
            return 0

        lax.fori_loop(0, RATIO, grid_body, 0)
        for off in range(1, n):
            to_blocks(off, lax.rem(me + off, n), me).start()
        r["hin"][pl.ds(2 * me, 2)] = r["mcur"][:, pl.ds(pl.multiple_of(nblk * me, nblk), nblk), :]

        def self_body(q, _):
            base = pl.multiple_of(q * rows, rows)
            at = pl.ds(base, rows)
            pre[0][...] = dot(r["gl"][at, :], r["wself"][0])
            act(pre[0], rows, hid[0])
            ys[0][...] = dot(hid[0][...], r["wself"][1])

            def store(o, v):
                w = pl.ds(base + o, SLAB)
                r["gcur"][w, :] = (r["gl"][w, :].astype(F32) + v).astype(BF16)

            finish(ys[0], rows, store)
            return 0

        lax.fori_loop(0, RATIO, self_body, 0)

        def copy_body(i, _):
            at = pl.ds(pl.multiple_of(i * chunk, chunk), chunk)
            r["e"][at, :] = r["ebase"][at, :]
            return 0

        lax.fori_loop(0, nchunk, copy_body, 0)
        for off in range(1, n):
            to_blocks(off, lax.rem(me + off, n), lax.rem(me + n - off, n)).wait()
        r["h"][...] = dot(r["pfwd"][...], r["hin"][...].reshape(rows, latent)).astype(BF16)

        lax.fori_loop(0, layers, layer_body, s * layers)

        r["yout"][...] = dot(r["pbwd"][...], r["h"][...]).astype(BF16).reshape(cols_j, nblk, latent)
        for off in range(1, n):
            to_grid(off, lax.rem(me + off, n), me).start()
        r["hb"][:, pl.ds(pl.multiple_of(nblk * me, nblk), nblk), :] = r["yout"][pl.ds(2 * me, 2)]
        for off in range(1, n):
            to_grid(off, lax.rem(me + off, n), lax.rem(me + n - off, n)).wait()

        def dec_body(q, _):
            base = pl.multiple_of(q * rows, rows)
            at = pl.ds(base, rows)
            hid[1][...] = dot(r["ex"][...], r["hb"][q]).astype(BF16)
            pre[0][...] = dot(hid[1][...], r["wi"][1, latent:2 * latent, :]) + dot(r["gcur"][at, :], r["wi"][1, 2 * latent:, :])
            act(pre[0], rows, hid[0], lambda o: r["decst"][pl.ds(base + o, SLAB), :])
            ys[0][...] = dot(hid[0][...], r["wo"][1])

            def store_edge(o, v):
                hid[1][o:o + SLAB, :] = (r["m2g"][pl.ds(base + o, SLAB), :].astype(F32) + v).astype(BF16)

            finish(ys[0], rows, store_edge)
            pre[1][...] = dot(r["gcur"][at, :], r["ni"][1, 0:latent, :]) + dot(hid[1][...], r["ni"][1, latent:, :])
            act(pre[1], rows, hid[0])
            ys[1][...] = dot(hid[0][...], r["no"][1])

            def store_node(o, v):
                hid[1][o:o + SLAB, :] = (r["gcur"][pl.ds(base + o, SLAB), :].astype(F32) + v).astype(BF16)

            finish(ys[1], rows, store_node)
            pre[0][...] = dot(hid[1][...], r["woh"][...])
            act(pre[0], rows, hid[0])
            pred = dot_bt(r["wof"][...], hid[0][...])
            x_prev[:, at] = x_cur[:, at] + dstd * pred[0:nvar] + dmean
            return 0

        lax.fori_loop(0, RATIO, dec_body, 0)
        pltpu.make_async_copy(x_prev, r["out"].at[s], r["out_sem"].at[s]).start()
        return 0

    lax.fori_loop(0, 2, step_body, 0)
    for s in range(2):
        pltpu.make_async_copy(r["xs"].at[s], r["out"].at[s], r["out_sem"].at[s]).wait()
    for c in fetch(1, (2 * layers) % 2):
        c.wait()


def solution(mesh):
    n = mesh.shape["gp"]
    row_spec = P(("dp", "gp"))
    edge_spec = P(("dp", "gp"), None, None)
    whole = P()

    def local_run(x_prev, x_cur, forcing, grid_static, g2m_feat, m2g_feat, mesh_feat, mesh_edge_feat, norm_stats, w_grid_in, w_mesh_in, w_eemb_in, w_embed_out, w_edge_in, w_edge_out, w_node_in, w_node_out, w_grid_self, w_out_hidden, w_out_final):
        grid_rows, nvar = x_prev.shape
        rows = mesh_feat.shape[0]
        latent = w_embed_out.shape[-1]
        blocks = w_edge_in.shape[0]
        in_feat = w_grid_in.shape[0]
        shift = rows // 2
        cols_j = n * rows // shift
        nblk = shift // n
        chunk = 2 * OFFSETS * cols_j

        def padded(a, count, axis=0):
            widths = [(0, 0)] * a.ndim
            widths[axis] = (0, count - a.shape[axis])
            return jnp.pad(a, widths)

        fs = jnp.concatenate([forcing.transpose(1, 2, 0), jnp.broadcast_to(grid_static.T[None], (2, grid_static.shape[1], grid_rows))], axis=1)
        gm = jnp.stack([padded(g2m_feat.T.astype(BF16), 16), padded(m2g_feat.T.astype(BF16), 16)])
        edge_t = mesh_edge_feat.transpose(1, 2, 0).reshape(-1, rows).astype(BF16)
        mf = jnp.concatenate([padded(edge_t, 32), padded(mesh_feat.T.astype(BF16), 16)])
        ew = jnp.concatenate([padded(w_mesh_in, 16)[None], padded(w_eemb_in, 16, 1)])
        wof = padded(w_out_final.T, 256)
        inputs = dict(xp_h=x_prev.T, xc_h=x_cur.T, fs_h=fs, ns_h=norm_stats.T, gm_h=gm, mf_h=mf, ew_h=ew, wg_h=w_grid_in, wemb_h=w_embed_out, wei_h=w_edge_in, weo_h=w_edge_out, wni_h=w_node_in, wno_h=w_node_out, wself_h=w_grid_self, woh_h=w_out_hidden, wof_h=wof)
        big = max(rows, chunk)
        vm = pltpu.VMEM
        dma = pltpu.SemaphoreType.DMA
        scratch = dict(
            xs=vm((2, nvar, grid_rows), F32), fs=vm(fs.shape, F32), ns=vm((nvar, 4), F32), gm=vm(gm.shape, BF16), mf=vm(mf.shape, BF16),
            ew=vm(ew.shape, BF16), wg=vm((rows, latent), BF16), wemb=vm(w_embed_out.shape, BF16),
            wi=vm((2, 3 * latent, latent), BF16), wo=vm((2, latent, latent), BF16), ni=vm((2, 2 * latent, latent), BF16), no=vm((2, latent, latent), BF16),
            wself=vm(w_grid_self.shape, BF16), woh=vm(w_out_hidden.shape, BF16), wof=vm(wof.shape, BF16),
            lwi=vm((2, 3 * latent, latent), BF16), lwo=vm((2, latent, latent), BF16), lni=vm((2, 2 * latent, latent), BF16), lno=vm((2, latent, latent), BF16),
            pfwd=vm((rows, rows), BF16), pbwd=vm((rows, rows), BF16), ex=vm((rows, rows // 2), BF16), ps=vm((rows // 2, rows), BF16),
            feat=vm((2, rows // 2, 128), BF16), fin=vm((cols_j, nblk, 128), BF16), featm=vm((rows, 128), BF16), mfp=vm((16, rows), BF16), g2p=vm((16, grid_rows), BF16),
            m2g=vm((grid_rows, latent), BF16), g2m=vm((grid_rows, latent), BF16), mlat=vm((rows, latent), BF16),
            decst=vm((grid_rows, latent), F32), encst=vm((grid_rows, latent), F32), nodst=vm((rows, latent), F32),
            gl=vm((grid_rows, latent), BF16), gcur=vm((grid_rows, latent), BF16), mcur=vm((2, rows // 2, latent), BF16),
            hin=vm((cols_j, nblk, latent), BF16), hb=vm((2, rows // 2, latent), BF16), yout=vm((cols_j, nblk, latent), BF16),
            ebase=vm((OFFSETS * rows, latent), BF16), e=vm((OFFSETS * rows, latent), BF16), h=vm((rows, latent), BF16),
            s0=vm((rows + 2 * cols_j, latent), F32), sup=vm((rows, latent), F32), sdn=vm((rows, latent), F32), rr=vm((rows, latent), F32), n1=vm((rows, latent), F32),
            esum=vm((rows, latent), BF16), halo=vm((2, 2, cols_j, latent), F32),
            p0=vm((big, latent), F32), p1=vm((big, latent), F32), h0=vm((big, latent), BF16), h1=vm((big, latent), BF16), y0=vm((big, latent), F32), y1=vm((big, latent), F32),
            load_sem=dma((20,)), fetch_sem=dma((2, 4)), out_sem=dma((2,)), fsend=dma((n, 2)), frecv=dma((n, 2)), nsend=dma((2,)), nrecv=dma((2,)),
            asend=dma((n,)), arecv=dma((n,)), bsend=dma((n,)), brecv=dma((n,)), hsend=dma((2,)), hrecv=dma((2, 2)),
        )
        cfg = dict(names=(*inputs, "out", *scratch), n=n, rows=rows, latent=latent, shift=shift, layers=blocks - 2, nvar=nvar, in_feat=in_feat)
        anywhere = pl.BlockSpec(memory_space=pl.ANY)
        out = pl.pallas_call(
            functools.partial(kernel, cfg),
            out_shape=jax.ShapeDtypeStruct((2, nvar, grid_rows), F32),
            in_specs=[anywhere] * len(inputs),
            out_specs=anywhere,
            scratch_shapes=list(scratch.values()),
            compiler_params=pltpu.CompilerParams(collective_id=0, has_side_effects=True, vmem_limit_bytes=66_000_000),
        )(*inputs.values())
        return out[0].T, out[1].T

    in_specs = (row_spec, row_spec, edge_spec, row_spec, row_spec, row_spec, row_spec, edge_spec, whole) + (whole,) * 11
    return jax.shard_map(local_run, mesh=mesh, in_specs=in_specs, out_specs=(row_spec, row_spec), check_vma=False)
```

time: 2320 us -> 374 us (0.16)
  matrix products: 745 us -> 0 us
  waiting for transfers between devices: 563 us -> 0 us
  other arithmetic: 366 us -> 6.21 us
  Pallas kernels: 0 us -> 356 us
  local copies, waits for them, and re-layouts: 357 us -> 8.35 us
  starting transfers between devices: 273 us -> 0 us
    dot_general x187 -> x0, matrix products: 745 us -> none  [the longest x186 737 us: matmul_f32(): return jnp.dot(values, weight, preferred_element_type=jnp.float32)]
    ppermute x132 -> x0, waiting for transfers between devices: 563 us -> none  [the longest x32 558 us: local_run(): lax.ppermute(mesh_cur[mesh_dev - half_shard:], 'gp', shift_pairs(1))]
    pallas_call x0 -> x1, Pallas kernels: none -> 356 us  [local_run(): pl.pallas_call(functools.partial(kernel, cfg), out_shape=jax.ShapeDtypeSt...]
    reduce_sum x114 -> x0, other arithmetic: 335 us -> none  [the longest x32 184 us: local_run(): edge_sum = jnp.sum(edge_lat, axis=1, dtype=jnp.float32).astype(jnp.bfloat16)]
    ppermute x132 -> x0, starting transfers between devices: 273 us -> none  [the longest x32 135 us: local_run(): far_plus = lax.ppermute(mesh_cur, 'gp', shift_pairs(-quarter_hop))]
    unnamed x471 -> x2, local copies, waits for them, and re-layouts: 275 us -> 2.26 us
    another operation x32 -> x1, local copies, waits for them, and re-layouts: 33.6 us -> 0.01 us  [local_run(): jnp.stack([padded(g2m_feat.T.astype(BF16), 16), padded(m2g_feat.T.astype(...]
    concatenate x32 -> x0, local copies, waits for them, and re-layouts: 25.2 us -> none  [local_run(): jnp.concatenate([prev_tail, mesh_cur, next_head, far_plus, far_minus], ax...]
  transfers between devices with their start and end apart: 132 -> 0, of which waited for: 37 -> 0; matrix products, arithmetic and copies ran while one was open for 12% -> 0% of each run, Pallas kernels for 0% -> 0%
where the time goes in v1:
time: 374 us; the launch traced here: 372 us
  Pallas kernels  356 us (95%)
  local copies, waits for them, and re-layouts  8.35 us (2%)
  other arithmetic  6.21 us (2%)
    pallas_call x1, Pallas kernels, local_run(): pl.pallas_call(functools.partial(kernel, cfg), out_shape=jax.ShapeDtypeSt...  356 us

profile of v1, /device:TPU:21, one launch (start us, length us, event | category | flops | bytes accessed | tf_op | source)
XLA Modules:
  0.0 371.7 jit_solution(6371458985853639539)
XLA Ops:
  0.6 0.7 convert_bitcast_fusion.3
  1.3 0.7 convert_bitcast_fusion.2
  2.1 0.7 convert_bitcast_fusion.1
  2.8 0.7 pad_bitcast_fusion.2
  3.5 0.8 convert_bitcast_fusion
  4.3 0.6 fusion.4.refs_5_
  4.9 1.3 fusion.3.refs_6_
  6.3 0.6 pad_maximum_fusion.1.refs_4_
  6.9 0.8 copy.25
  7.7 0.8 broadcast_in_dim.4
  8.5 0.7 pad_maximum_fusion.refs_2_
  9.1 1.5 copy.23
  10.6 1.7 pad.32.refs_15_
  12.3 356.5 %shard_map.203 = f32[2,227,1024]{2,1,0:T(8,128)} custom-call(f32[227,1024]{1,0:T(8,128)} %bitcast.30, f32[227,1024]{1,0:T(8,128)} %bitcast.31, f32[2,10,1024]{2,1,0:T(8,128)} %pad_maximum_fusion.refs_2_, f32[227,4]{1,0:T(8,128)} %bitcast.32, bf16[2,16,1024]{2,1,0:T(8,128)(2,1)} %pad_maximum_fusion.1.refs_4_, bf16[48,512]{1,0:T(8,128)(2,1)} %fusion.4.refs_5_, ...), custom_call_target="tpu_custom_call" | custom-call | tf_op jit(solution)/shard_map/pallas_call | solution.py:501
  368.7 3.0 slice_bitcast_fusion
  (2 shorter events, 0.0 us)

commit v2 on v0

v2 whole, which is shorter than its diff:
```python
import functools
import types

import jax
import jax.numpy as jnp
from jax import lax
from jax.experimental import pallas as pl
from jax.experimental.pallas import tpu as pltpu
from jax.sharding import PartitionSpec as P

F32 = jnp.float32
BF16 = jnp.bfloat16
SLAB = 16
RATIO = 2
OFFSETS = 6
LOWER = ("E6", "A7", "S7", "F0", "F1", "A0", "nf1", "E7", "na1", "nf2", "na2", "A1", "ns2", "S0", "F3", "F2", "ne2", "ns1", "ne1", "S1", "E0", "A2", "E1", "S2", "ps2")
UPPER = ("ro2", "ps1", "E2", "ro1", "pr1", "A3", "S3", "pr2", "F4", "A4", "E3", "F5", "S4", "nf0", "A5", "F6", "na0", "S5", "ns0", "E4", "A6", "ne0", "KEEP", "E5", "S6", "F7", "ps0", "ro0", "pr0")


def dot(a, b):
    return jnp.dot(a, b, preferred_element_type=F32)


def dot_t(a, b):
    return lax.dot_general(a, b, (((0,), (0,)), ((), ())), preferred_element_type=F32)


def dot_bt(a, b):
    return lax.dot_general(a, b, (((1,), (1,)), ((), ())), preferred_element_type=F32)


def silu(x):
    return x * lax.logistic(x)


def layer_norm(y):
    centred = y - jnp.mean(y, axis=-1, keepdims=True)
    spread = jnp.mean(centred * centred, axis=-1, keepdims=True)
    return centred * lax.rsqrt(spread + 1e-5)


def kernel(cfg, *refs):
    r = types.SimpleNamespace(**dict(zip(cfg.names, refs, strict=True)))
    n, rows, latent, shift, layers = cfg.n, cfg.rows, cfg.latent, cfg.shift, cfg.layers
    nvar, in_feat = cfg.nvar, cfg.in_feat
    cols_j = n * rows // shift
    nblk = shift // n
    quarter = cols_j // 4
    grid_rows = RATIO * rows
    per_blk = OFFSETS * cols_j
    bpc = 2
    chunk = bpc * per_blk
    nchunk = nblk // bpc
    pair = nblk // 2
    chunks = [(2 * i + 1, 2 * i + 2) for i in range(pair // 2 - 1)] + [(0, pair - 1)] + [(pair + 2 * i, pair + 2 * i + 1) for i in range(pair // 2)]
    flat = [p for c in chunks for p in c]
    me = lax.axis_index("gp")
    left = lax.rem(me + n - 1, n)
    right = lax.rem(me + 1, n)
    pre, hid, ys = (r.p0, r.p1), (r.h0, r.h1), (r.y0, r.y1)

    def remote(src, dst, send, recv, dev):
        return pltpu.make_async_remote_copy(src_ref=src, dst_ref=dst, send_sem=send, recv_sem=recv, device_id={"gp": dev}, device_id_type=pl.DeviceIdType.MESH)

    last = layers + 1
    pairs = dict(
        mfr=(r.mf_h, r.mfr), mer=(r.me_h, r.mer), g2r=(r.g2_h, r.g2r), m2r=(r.m2_h, r.m2r), gsr=(r.gs_h, r.gsr), frr=(r.fr_h, r.frr), nsr=(r.ns_h, r.nsr),
        wmr=(r.wm_h, r.wmr), wer=(r.we_h, r.wer), xp=(r.xp_h, r.xs.at[0]), xc=(r.xc_h, r.xs.at[1]), wg=(r.wg_h, r.wg.at[0:in_feat]), wemb=(r.wemb_h, r.wemb),
        wi1=(r.wei_h.at[last], r.wi.at[1]), wi0=(r.wei_h.at[0], r.wi.at[0]), ni0=(r.wni_h.at[0], r.ni.at[0]), wo0=(r.weo_h.at[0], r.wo.at[0]), no0=(r.wno_h.at[0], r.no.at[0]),
        wself=(r.wself_h, r.wself), wo1=(r.weo_h.at[last], r.wo.at[1]), ni1=(r.wni_h.at[last], r.ni.at[1]), no1=(r.wno_h.at[last], r.no.at[1]), woh=(r.woh_h, r.woh), wof=(r.wof_h, r.wof),
    )
    load = types.SimpleNamespace(**{key: pltpu.make_async_copy(src, dst, r.load_sem.at[i]) for i, (key, (src, dst)) in enumerate(pairs.items())})

    def fetch(layer, slot):
        pairs = ((r.wei_h, r.lwi), (r.weo_h, r.lwo), (r.wni_h, r.lni), (r.wno_h, r.lno))
        return [pltpu.make_async_copy(src.at[layer], dst.at[slot], r.fetch_sem.at[slot, i]) for i, (src, dst) in enumerate(pairs)]

    for c in vars(load).values():
        c.start()
    for c in fetch(1, 0):
        c.start()

    barrier = pltpu.get_barrier_semaphore()
    for off in range(1, n):
        pl.semaphore_signal(barrier, inc=1, device_id={"gp": lax.rem(me + off, n)}, device_id_type=pl.DeviceIdType.MESH)

    def iota(shape, dim):
        return lax.broadcasted_iota(jnp.int32, shape, dim)

    def onehot(pred):
        return jnp.where(pred, 1.0, 0.0).astype(BF16)

    def slot_of(row):
        jp = lax.rem(lax.rem(row, cols_j) + (cols_j - 1), cols_j)
        return jp * nblk + lax.rem(lax.div(row, cols_j) + 1, nblk)

    for t in range(rows // 128):
        sl = slice(128 * t, 128 * t + 128)
        r.pfwd[sl, :] = onehot(iota((128, rows), 1) == slot_of(iota((128, rows), 0) + 128 * t))
        r.pbwd[sl, :] = onehot(iota((128, rows), 0) + 128 * t == slot_of(iota((128, rows), 1)))
    half = rows // 2
    r.ex[...] = onehot(lax.div(iota((rows, half), 0), RATIO) == iota((rows, half), 1))
    r.ps[...] = onehot(iota((half, rows), 0) == lax.div(iota((half, rows), 1), RATIO))
    for ref in (r.s0, r.sup, r.sdn, r.rr, r.n1, r.edge_s, r.keep, r.esum):
        ref[...] = jnp.zeros(ref.shape, ref.dtype)
    r.wg[in_feat:, :] = jnp.zeros((r.wg.shape[0] - in_feat, latent), BF16)

    def act(p, count, hidden, add=None):
        for o in range(0, count, SLAB):
            x = p[o:o + SLAB, :]
            if add is not None:
                x = x + add(o)
            hidden[o:o + SLAB, :] = silu(x).astype(BF16)

    def finish(y, count, store):
        for o in range(0, count, SLAB):
            store(o, layer_norm(y[o:o + SLAB, :]))

    st = r.p0
    wide = grid_rows // latent

    def staged(value, count=16):
        st[0:count, :] = jnp.zeros((count, latent), F32)
        st[0:value.shape[0], :] = value.astype(F32)
        return st[0:count, :].astype(BF16)

    for c in (load.mfr, load.mer, load.g2r, load.m2r, load.gsr, load.frr, load.nsr, load.wmr, load.wer):
        c.wait()
    r.ew[0] = staged(r.wmr[...])
    for i in range(3):
        r.ew[i + 1] = staged(r.wer[i])
    for i in range(wide):
        at = slice(i * latent, (i + 1) * latent)
        r.gm[0, :, at] = staged(r.g2r[:, at])
        r.gm[1, :, at] = staged(r.m2r[:, at])
    r.mf[32:48, :] = staged(r.mfr[...])
    st[0:32, :] = jnp.zeros((32, latent), F32)
    for k in range(OFFSETS):
        st[4 * k:4 * k + 4, :] = r.mer[k]
    r.mf[0:32, :] = st[0:32, :].astype(BF16)
    force = r.frr.shape[0]
    for i in range(2):
        r.fs[i, 0:force, :] = r.frr[:, i, :]
        r.fs[i, force:force + r.gsr.shape[0], :] = r.gsr[...]
    st[0:128, :] = jnp.zeros((128, latent), F32)
    st[0:4, 0:nvar] = r.nsr[...]
    r.ns[...] = jnp.transpose(st[0:128, 0:256])
    eye = onehot(iota((32, 128), 0) == iota((32, 128), 1))
    r.feat[...] = dot_t(r.mf[0:32, :], eye).astype(BF16).reshape(2, half, 128)
    def grid_embed(s, base):
        at = pl.ds(base, rows)
        mean, std = (r.ns[0:nvar, i:i + 1] for i in (0, 1))
        p = r.p0
        p[0:nvar, :] = (r.xs[s, :, at] - mean) / std
        p[nvar:2 * nvar, :] = (r.xs[1 - s, :, at] - mean) / std
        p[2 * nvar:in_feat, :] = r.fs[s, 0:in_feat - 2 * nvar, at]
        p[in_feat:, :] = jnp.zeros((p.shape[0] - in_feat, rows), F32)
        r.h0[...] = p[...].astype(BF16)
        r.p1[...] = dot_t(r.h0[...], r.wg[...])
        act(r.p1, rows, r.h1)
        r.y1[...] = dot(r.h1[...], r.wemb[0])

        def store(o, v):
            r.gl[pl.ds(base + o, SLAB), :] = v.astype(BF16)

        finish(r.y1, rows, store)

    def first_embed(q, _):
        grid_embed(0, pl.multiple_of(q * rows, rows))
        return 0

    for c in (load.xp, load.xc, load.wg, load.wemb):
        c.wait()
    lax.fori_loop(0, RATIO, first_embed, 0)
    pl.semaphore_wait(barrier, n - 1)

    def feat_copy(off, jj, dev, owner):
        slot = lax.rem(2 * owner + jj + cols_j - 1, cols_j)
        return remote(r.feat.at[jj, pl.ds(pl.multiple_of(nblk * dev, nblk), nblk), :], r.fin.at[slot], r.fsend.at[off, jj], r.frecv.at[off, jj], dev)

    nb_copies = [
        remote(r.mf.at[32:48, 0:half], r.mfp.at[:, half:], r.nsend.at[0], r.nrecv.at[0], left),
        remote(r.gm.at[0, :, 0:rows], r.g2p.at[:, rows:], r.nsend.at[1], r.nrecv.at[1], left),
    ]
    for c in nb_copies:
        c.start()
    for off in range(1, n):
        for jj in range(2):
            feat_copy(off, jj, lax.rem(me + off, n), me).start()
    for jj in range(2):
        r.fin[lax.rem(2 * me + jj + cols_j - 1, cols_j)] = r.feat[jj, pl.ds(pl.multiple_of(nblk * me, nblk), nblk), :]
    r.mfp[:, 0:half] = r.mf[32:48, half:]
    r.g2p[:, 0:rows] = r.gm[0, :, rows:]


    def embed(lhs_t, w_first, w_second, store):
        r.p0[0:rows, :] = dot_t(lhs_t, w_first)
        act(r.p0, rows, r.h0)
        r.y0[0:rows, :] = dot(r.h0[0:rows, :], w_second)
        finish(r.y0, rows, store)

    load.wi1.wait()

    def m2g_body(q, _):
        base = pl.multiple_of(q * rows, rows)

        def store(o, v):
            r.m2g[pl.ds(base + o, SLAB), :] = v.astype(BF16)

        embed(r.gm[1, :, pl.ds(base, rows)], r.ew[2], r.wemb[3], store)
        r.decst[pl.ds(base, rows), :] = dot(r.m2g[pl.ds(base, rows), :], r.wi[1, 0:latent, :])
        return 0

    lax.fori_loop(0, RATIO, m2g_body, 0)

    for c in nb_copies:
        c.wait()
    load.wi0.wait()
    load.ni0.wait()

    def store_mesh(o, v):
        r.mlat[o:o + SLAB, :] = v.astype(BF16)

    embed(r.mfp[...], r.ew[0], r.wemb[1], store_mesh)
    r.nodst[...] = dot(r.mlat[...], r.ni[0, 0:latent, :])

    def g2m_body(q, _):
        base = pl.multiple_of(q * rows, rows)
        hbase = pl.multiple_of(q * half, half)

        def store(o, v):
            r.g2m[pl.ds(base + o, SLAB), :] = v.astype(BF16)

        embed(r.g2p[:, pl.ds(base, rows)], r.ew[1], r.wemb[2], store)
        r.h1[0:rows, :] = dot(r.ex[...], r.mlat[pl.ds(hbase, half), :]).astype(BF16)
        r.encst[pl.ds(base, rows), :] = dot(r.g2m[pl.ds(base, rows), :], r.wi[0, 0:latent, :]) + dot(r.h1[0:rows, :], r.wi[0, 2 * latent:, :])
        return 0

    lax.fori_loop(0, RATIO, g2m_body, 0)

    for c in (load.wo0, load.no0, load.wself):
        c.wait()

    def late_static():
        for c in (load.wo1, load.ni1, load.no1, load.woh, load.wof):
            c.wait()
        for off in range(1, n):
            for jj in range(2):
                feat_copy(off, jj, lax.rem(me + off, n), lax.rem(me + n - off, n)).wait()
        r.featm[...] = dot(r.pfwd[...], r.fin[...].reshape(rows, 128)).astype(BF16)

        def edge_body(k, _):
            sel = onehot(iota((128, 16), 0) == iota((128, 16), 1) + 4 * k)
            sel = jnp.where(iota((128, 16), 1) < 4, sel, jnp.zeros_like(sel))
            w_k = dot(sel, r.ew[3]).astype(BF16)
            r.p0[0:rows, :] = dot(r.featm[...], w_k)
            act(r.p0, rows, r.h0)
            r.y0[0:rows, :] = dot(r.h0[0:rows, :], r.wemb[4])

            def store(o, v):
                pos = flat.index(o // cols_j)
                at = pl.multiple_of(pos * per_blk + (o % cols_j // SLAB * OFFSETS + k) * SLAB, SLAB)
                r.ebase[pl.ds(at, SLAB), :] = v.astype(BF16)

            finish(r.y0, rows, store)
            return 0

        lax.fori_loop(0, OFFSETS, edge_body, 0)

    far_first = sorted(range(1, n), key=lambda off: -min(off, n - off))

    def to_blocks(off, q, dev, owner):
        return remote(r.mcur.at[q, pl.ds(pl.multiple_of(nblk * dev, nblk), nblk), :], r.hin.at[2 * owner + q], r.asend.at[off, q], r.arecv.at[off, q], dev)

    def to_grid(off, q, dev, owner):
        return remote(r.yout.at[2 * dev + q], r.hb.at[q, pl.ds(pl.multiple_of(nblk * owner, nblk), nblk), :], r.bsend.at[off, q], r.brecv.at[off, q], dev)

    s0, sup, sdn, rr, n1, e, h, esum = r.s0, r.sup, r.sdn, r.rr, r.n1, r.e, r.h, r.esum
    npre, nhid, nys = r.np, r.nh, r.ny
    group = rows // 2

    def halo_copies(par):
        lo, hi = (nblk - 2) * cols_j, (nblk - 1) * cols_j
        return [
            remote(s0.at[lo:lo + cols_j], r.halo.at[par, 0], r.hsend.at[0], r.hrecv.at[par, 0], right),
            remote(s0.at[hi:hi + cols_j], r.halo.at[par, 1], r.hsend.at[1], r.hrecv.at[par, 1], left),
        ]

    def take_halo(par):
        for c in halo_copies(par):
            c.wait()
        low, high = r.halo[par, 0], r.halo[par, 1]
        low_w = jnp.concatenate([low[-1:], low[:-1]], axis=0)
        high_w = jnp.concatenate([high[1:], high[:1]], axis=0)
        r.edge_s[0] = jnp.where(me == 0, low_w, low)
        r.edge_s[1] = jnp.where(me == n - 1, high_w, high)

    def send(p, k, g):
        at = slice(SLAB * g, SLAB * g + SLAB)
        if k == 0:
            if p == nblk - 2:
                return r.edge_s[1, at, :]
            if p == nblk - 1:
                return r.keep[at, :]
            base = (p + 1) % nblk * cols_j
            return s0[base + SLAB * g:base + SLAB * g + SLAB, :]
        if k == 1:
            if p == nblk - 1:
                return r.edge_s[0, at, :]
            base = (p - 1) % nblk * cols_j
            return s0[base + SLAB * g:base + SLAB * g + SLAB, :]
        base = p * cols_j
        if k in (2, 3):
            return (sup, sdn)[k - 2][base + SLAB * g:base + SLAB * g + SLAB, :]
        sh = quarter if k == 4 else -quarter
        lo, hi = (SLAB * g + sh) % cols_j, (SLAB * g + 8 + sh) % cols_j
        return jnp.concatenate([s0[base + lo:base + lo + 8, :], s0[base + hi:base + hi + 8, :]], axis=0)

    def edge_act(i):
        for bb, p in enumerate(chunks[i]):
            for g in range(cols_j // SLAB):
                recv = rr[p * cols_j + SLAB * g:p * cols_j + SLAB * g + SLAB, :]
                for k in range(OFFSETS):
                    o = bb * per_blk + (g * OFFSETS + k) * SLAB
                    hid[i % 2][o:o + SLAB, :] = silu(pre[i % 2][o:o + SLAB, :] + send(p, k, g) + recv).astype(BF16)

    def edge_finish(i):
        rows6 = OFFSETS * SLAB
        for bb, p in enumerate(chunks[i]):
            for g in range(cols_j // SLAB):
                o = bb * per_blk + g * rows6
                eo = i * chunk + o
                new = (e[eo:eo + rows6, :].astype(F32) + layer_norm(ys[i % 2][o:o + rows6, :])).astype(BF16)
                e[eo:eo + rows6, :] = new
                total = new[0:SLAB].astype(F32)
                for k in range(1, OFFSETS):
                    total = total + new[k * SLAB:(k + 1) * SLAB].astype(F32)
                esum[p * cols_j + SLAB * g:p * cols_j + SLAB * g + SLAB, :] = total.astype(BF16)

    def edge_first(i, wi):
        pre[i % 2][0:chunk, :] = dot(e[i * chunk:(i + 1) * chunk, :], wi[0:latent, :])

    def edge_second(i, wo):
        ys[i % 2][0:chunk, :] = dot(hid[i % 2][0:chunk, :], wo[...])

    groups = ((0, group), (group, group // 2), (group + group // 2, group // 2))

    def project_send(g, wi):
        o, count = groups[g]
        s0[o:o + count, :] = dot(h[o:o + count, :], wi[latent:2 * latent, :])

    def roll_send(g):
        o, count = groups[g]
        for at in range(o, o + count, cols_j):
            blk = s0[at:at + cols_j, :]
            sup[at:at + cols_j, :] = jnp.concatenate([blk[1:], blk[:1]], axis=0)
            sdn[at:at + cols_j, :] = jnp.concatenate([blk[-1:], blk[:-1]], axis=0)

    def project_rest(g, wi, ni):
        o, count = groups[g]
        rr[o:o + count, :] = dot(h[o:o + count, :], wi[2 * latent:, :])
        n1[o:o + count, :] = dot(h[o:o + count, :], ni[0:latent, :])

    def node_first(g, ni):
        o, count = groups[g]
        npre[o:o + count, :] = dot(esum[o:o + count, :], ni[latent:, :])

    def node_act(g):
        o, count = groups[g]
        for at in range(o, o + count, SLAB):
            nhid[at:at + SLAB, :] = silu(npre[at:at + SLAB, :] + n1[at:at + SLAB, :]).astype(BF16)

    def node_second(g, no):
        o, count = groups[g]
        nys[o:o + count, :] = dot(nhid[o:o + count, :], no[...])

    def node_finish(g):
        o, count = groups[g]
        step = 4 * SLAB
        for at in range(o, o + count, step):
            h[at:at + step, :] = (h[at:at + step, :].astype(F32) + layer_norm(nys[at:at + step, :])).astype(BF16)

    def weights(i):
        return [x.at[i] for x in (r.lwi, r.lwo, r.lni, r.lno)]

    def layer_body(t, first):
        cur, was, nxt = (lax.rem(first + t + i, 3) for i in (0, 2, 1))
        par = lax.rem(first + t, 2)
        wi, wo, ni, no = weights(cur)
        wi_n, _, ni_n, _ = weights(nxt)
        _, wo_w, ni_w, no_w = weights(was)

        @pl.when(t > 0)
        def _():
            take_halo(1 - par)

        def run(stages, table):
            for stage in stages:
                name = stage.rstrip("0123456789")
                table[name](*(int(d) for d in stage[len(name):]))

        last_chunk = nchunk - 1
        run(LOWER, dict(
            A=edge_act, E=edge_finish, F=lambda i: edge_first(i, wi), S=lambda i: edge_second(i, wo_w if i == last_chunk else wo),
            nf=lambda g: node_first(g, ni_w), na=node_act, ns=lambda g: node_second(g, no_w), ne=node_finish,
            ps=lambda g: project_send(g, wi), ro=roll_send))
        for c in halo_copies(par):
            c.start()
        for c in fetch(jnp.where(t + 1 < layers, t + 2, 1), nxt):
            c.wait()
        for c in fetch(jnp.where(t + 2 < layers, t + 3, t + 3 - layers), was):
            c.start()

        def keep():
            r.keep[...] = s0[0:cols_j, :]

        run(UPPER, dict(
            A=edge_act, E=edge_finish, F=lambda i: edge_first(i, wi), S=lambda i: edge_second(i, wo),
            nf=lambda g: node_first(g, ni), na=node_act, ns=lambda g: node_second(g, no), ne=node_finish,
            ps=lambda g: project_send(g, wi if g else wi_n), pr=lambda g: project_rest(g, wi if g else wi_n, ni if g else ni_n), ro=roll_send, KEEP=keep))
        return first

    def run_layers(first):
        was, cur = (lax.rem(first + i, 3) for i in (2, 0))
        wi, _, ni, _ = weights(cur)
        r.lwo[was] = jnp.zeros((latent, latent), BF16)
        r.lno[was] = jnp.zeros((latent, latent), BF16)
        r.lni[was, latent:, :] = jnp.zeros((latent, latent), BF16)
        r.y0[...] = jnp.zeros(r.y0.shape, F32)
        project_send(0, wi)
        roll_send(0)
        project_rest(0, wi, ni)
        lax.fori_loop(0, layers, layer_body, first)
        was = lax.rem(first + layers + 2, 3)
        take_halo(lax.rem(first + layers + 1, 2))
        edge_act(7)
        edge_second(7, r.lwo.at[was])
        edge_finish(6)
        edge_finish(7)
        for g in (1, 2):
            node_first(g, r.lni.at[was])
            node_act(g)
            node_second(g, r.lno.at[was])
            node_finish(g)

    def step_body(s, _):
        x_prev, x_cur = r.xs.at[s], r.xs.at[1 - s]
        dmean, dstd = (r.ns[0:nvar, i:i + 1] for i in (2, 3))

        def grid_body(q, _):
            base = pl.multiple_of(q * rows, rows)
            at = pl.ds(base, rows)

            @pl.when(s > 0)
            def _():
                grid_embed(s, base)

            r.p0[...] = dot(r.gl[at, :], r.wi[0, latent:2 * latent, :])
            act(r.p0, rows, r.h0, lambda o: r.encst[pl.ds(base + o, SLAB), :])
            r.y0[...] = dot(r.h0[...], r.wo[0])

            def store_edge(o, v):
                r.h1[o:o + SLAB, :] = (r.g2m[pl.ds(base + o, SLAB), :].astype(F32) + v).astype(BF16)

            finish(r.y0, rows, store_edge)
            hbase = pl.multiple_of(q * half, half)
            esum = dot(r.ps[...], r.h1[...]).astype(BF16)
            r.p1[0:half, :] = dot(esum, r.ni[0, latent:, :])
            act(r.p1, half, r.h0, lambda o: r.nodst[pl.ds(hbase + o, SLAB), :])
            r.y1[0:half, :] = dot(r.h0[0:half, :], r.no[0])

            def store_node(o, v):
                r.mcur[q, o:o + SLAB, :] = (r.mlat[pl.ds(hbase + o, SLAB), :].astype(F32) + v).astype(BF16)

            finish(r.y1, half, store_node)
            for off in far_first:
                to_blocks(off, q, lax.rem(me + off, n), me).start()
            r.hin[2 * me + q] = r.mcur[q, pl.ds(pl.multiple_of(nblk * me, nblk), nblk), :]
            return 0

        lax.fori_loop(0, RATIO, grid_body, 0)
        def self_body(q, _):
            base = pl.multiple_of(q * rows, rows)
            at = pl.ds(base, rows)
            r.p0[...] = dot(r.gl[at, :], r.wself[0])
            act(r.p0, rows, r.h0)
            r.y0[...] = dot(r.h0[...], r.wself[1])

            def store(o, v):
                w = pl.ds(base + o, SLAB)
                r.gcur[w, :] = (r.gl[w, :].astype(F32) + v).astype(BF16)

            finish(r.y0, rows, store)
            return 0

        lax.fori_loop(0, RATIO, self_body, 0)
        pl.when(s == 0)(late_static)

        def copy_body(i, _):
            at = pl.ds(pl.multiple_of(i * chunk, chunk), chunk)
            r.e[at, :] = r.ebase[at, :]
            return 0

        lax.fori_loop(0, nchunk, copy_body, 0)
        for q in range(2):
            for off in far_first:
                to_blocks(off, q, lax.rem(me + off, n), lax.rem(me + n - off, n)).wait()
        r.h[...] = dot(r.pfwd[...], r.hin[...].reshape(rows, latent)).astype(BF16)

        run_layers(s * layers)

        r.yout[...] = dot(r.pbwd[...], r.h[...]).astype(BF16).reshape(cols_j, nblk, latent)
        for q in range(2):
            for off in far_first:
                to_grid(off, q, lax.rem(me + off, n), me).start()
        for q in range(2):
            r.hb[q, pl.ds(pl.multiple_of(nblk * me, nblk), nblk), :] = r.yout[2 * me + q]

        def dec_body(q, _):
            base = pl.multiple_of(q * rows, rows)
            at = pl.ds(base, rows)
            for off in far_first:
                to_grid(off, q, lax.rem(me + off, n), lax.rem(me + n - off, n)).wait()
            r.h1[...] = dot(r.ex[...], r.hb[q]).astype(BF16)
            r.p0[...] = dot(r.h1[...], r.wi[1, latent:2 * latent, :]) + dot(r.gcur[at, :], r.wi[1, 2 * latent:, :])
            act(r.p0, rows, r.h0, lambda o: r.decst[pl.ds(base + o, SLAB), :])
            r.y0[...] = dot(r.h0[...], r.wo[1])

            def store_edge(o, v):
                r.h1[o:o + SLAB, :] = (r.m2g[pl.ds(base + o, SLAB), :].astype(F32) + v).astype(BF16)

            finish(r.y0, rows, store_edge)
            r.p1[...] = dot(r.gcur[at, :], r.ni[1, 0:latent, :]) + dot(r.h1[...], r.ni[1, latent:, :])
            act(r.p1, rows, r.h0)
            r.y1[...] = dot(r.h0[...], r.no[1])

            def store_node(o, v):
                r.h1[o:o + SLAB, :] = (r.gcur[pl.ds(base + o, SLAB), :].astype(F32) + v).astype(BF16)

            finish(r.y1, rows, store_node)
            r.p0[...] = dot(r.h1[...], r.woh[...])
            act(r.p0, rows, r.h0)
            pred = dot_bt(r.wof[...], r.h0[...])
            x_prev[:, at] = x_cur[:, at] + dstd * pred + dmean
            return 0

        lax.fori_loop(0, RATIO, dec_body, 0)
        pltpu.make_async_copy(x_prev, r.out.at[s], r.out_sem.at[s]).start()
        return 0

    for c in fetch(1, 0):
        c.wait()
    for c in fetch(2, 1):
        c.start()
    lax.fori_loop(0, 2, step_body, 0)
    for s in range(2):
        pltpu.make_async_copy(r.xs.at[s], r.out.at[s], r.out_sem.at[s]).wait()
    for c in fetch(1, (2 * layers + 1) % 3):
        c.wait()


def solution(mesh):
    n = mesh.shape["gp"]
    row_spec = P(("dp", "gp"))
    edge_spec = P(("dp", "gp"), None, None)
    whole = P()

    def local_run(x_prev, x_cur, forcing, grid_static, g2m_feat, m2g_feat, mesh_feat, mesh_edge_feat, norm_stats, w_grid_in, w_mesh_in, w_eemb_in, w_embed_out, w_edge_in, w_edge_out, w_node_in, w_node_out, w_grid_self, w_out_hidden, w_out_final):
        grid_rows, nvar = x_prev.shape
        rows = mesh_feat.shape[0]
        latent = w_embed_out.shape[-1]
        blocks = w_edge_in.shape[0]
        in_feat = w_grid_in.shape[0]
        shift = rows // 2
        cols_j = n * rows // shift
        nblk = shift // n
        chunk = 2 * OFFSETS * cols_j

        inputs = dict(xp_h=x_prev.T, xc_h=x_cur.T, fr_h=forcing.transpose(2, 1, 0), gs_h=grid_static.T, g2_h=g2m_feat.T, m2_h=m2g_feat.T, mf_h=mesh_feat.T, me_h=mesh_edge_feat.transpose(1, 2, 0), ns_h=norm_stats, wm_h=w_mesh_in, we_h=w_eemb_in, wg_h=w_grid_in, wemb_h=w_embed_out, wei_h=w_edge_in, weo_h=w_edge_out, wni_h=w_node_in, wno_h=w_node_out, wself_h=w_grid_self, woh_h=w_out_hidden, wof_h=w_out_final.T)
        big = max(rows, chunk)
        vm = pltpu.VMEM
        dma = pltpu.SemaphoreType.DMA
        scratch = dict(
            xs=vm((2, nvar, grid_rows), F32), fs=vm((2, 16, grid_rows), F32), ns=vm((256, 128), F32), gm=vm((2, 16, grid_rows), BF16), mf=vm((48, rows), BF16),
            ew=vm((4, 16, latent), BF16), wg=vm((rows, latent), BF16), wemb=vm(w_embed_out.shape, BF16),
            wi=vm((2, 3 * latent, latent), BF16), wo=vm((2, latent, latent), BF16), ni=vm((2, 2 * latent, latent), BF16), no=vm((2, latent, latent), BF16),
            wself=vm(w_grid_self.shape, BF16), woh=vm(w_out_hidden.shape, BF16),
            lwi=vm((3, 3 * latent, latent), BF16), lwo=vm((3, latent, latent), BF16), lni=vm((3, 2 * latent, latent), BF16), lno=vm((3, latent, latent), BF16),
            pfwd=vm((rows, rows), BF16), pbwd=vm((rows, rows), BF16), ex=vm((rows, rows // 2), BF16), ps=vm((rows // 2, rows), BF16),
            feat=vm((2, rows // 2, 128), BF16), fin=vm((cols_j, nblk, 128), BF16), featm=vm((rows, 128), BF16), mfp=vm((16, rows), BF16), g2p=vm((16, grid_rows), BF16),
            m2g=vm((grid_rows, latent), BF16), g2m=vm((grid_rows, latent), BF16), mlat=vm((rows, latent), BF16),
            decst=vm((grid_rows, latent), F32), encst=vm((grid_rows, latent), F32), nodst=vm((rows, latent), F32),
            gl=vm((grid_rows, latent), BF16), gcur=vm((grid_rows, latent), BF16), mcur=vm((2, rows // 2, latent), BF16),
            hin=vm((cols_j, nblk, latent), BF16), hb=vm((2, rows // 2, latent), BF16), yout=vm((cols_j, nblk, latent), BF16),
            ebase=vm((OFFSETS * rows, latent), BF16), e=vm((OFFSETS * rows, latent), BF16), h=vm((rows, latent), BF16),
            s0=vm((rows, latent), F32), sup=vm((rows, latent), F32), sdn=vm((rows, latent), F32), rr=vm((rows, latent), F32), n1=vm((rows, latent), F32),
            esum=vm((rows, latent), BF16), edge_s=vm((2, cols_j, latent), F32), keep=vm((cols_j, latent), F32), np=vm((rows, latent), F32), nh=vm((rows, latent), BF16), ny=vm((rows, latent), F32), halo=vm((2, 2, cols_j, latent), F32),
            p0=vm((big, latent), F32), p1=vm((big, latent), F32), h0=vm((big, latent), BF16), h1=vm((big, latent), BF16), y0=vm((big, latent), F32), y1=vm((big, latent), F32),
            wof=vm((nvar, latent), BF16), mfr=vm((mesh_feat.shape[1], rows), F32), mer=vm((*mesh_edge_feat.shape[1:], rows), F32), g2r=vm((g2m_feat.shape[1], grid_rows), F32), m2r=vm((m2g_feat.shape[1], grid_rows), F32),
            gsr=vm((grid_static.shape[1], grid_rows), F32), frr=vm((forcing.shape[2], forcing.shape[1], grid_rows), F32), nsr=vm(norm_stats.shape, F32), wmr=vm(w_mesh_in.shape, BF16), wer=vm(w_eemb_in.shape, BF16),
            load_sem=dma((24,)), fetch_sem=dma((3, 4)), out_sem=dma((2,)), fsend=dma((n, 2)), frecv=dma((n, 2)), nsend=dma((2,)), nrecv=dma((2,)),
            asend=dma((n, 2)), arecv=dma((n, 2)), bsend=dma((n, 2)), brecv=dma((n, 2)), hsend=dma((2,)), hrecv=dma((2, 2)),
        )
        cfg = types.SimpleNamespace(names=(*inputs, "out", *scratch), n=n, rows=rows, latent=latent, shift=shift, layers=blocks - 2, nvar=nvar, in_feat=in_feat)
        anywhere = pl.BlockSpec(memory_space=pl.ANY)
        out = pl.pallas_call(
            functools.partial(kernel, cfg),
            out_shape=jax.ShapeDtypeStruct((2, nvar, grid_rows), F32),
            in_specs=[anywhere] * len(inputs),
            out_specs=anywhere,
            scratch_shapes=list(scratch.values()),
            compiler_params=pltpu.CompilerParams(collective_id=0, has_side_effects=True, vmem_limit_bytes=66_000_000),
        )(*inputs.values())
        return out[0].T, out[1].T

    in_specs = (row_spec, row_spec, edge_spec, row_spec, row_spec, row_spec, row_spec, edge_spec, whole) + (whole,) * 11
    return jax.shard_map(local_run, mesh=mesh, in_specs=in_specs, out_specs=(row_spec, row_spec), check_vma=False)
```

time: 2320 us -> 289 us (0.12)
  matrix products: 745 us -> 0 us
  waiting for transfers between devices: 563 us -> 0 us
  other arithmetic: 366 us -> 0 us
  local copies, waits for them, and re-layouts: 357 us -> 2.95 us
  Pallas kernels: 0 us -> 285 us
  starting transfers between devices: 273 us -> 0 us
    dot_general x187 -> x0, matrix products: 745 us -> none  [the longest x186 737 us: matmul_f32(): return jnp.dot(values, weight, preferred_element_type=jnp.float32)]
    ppermute x132 -> x0, waiting for transfers between devices: 563 us -> none  [the longest x32 558 us: local_run(): lax.ppermute(mesh_cur[mesh_dev - half_shard:], 'gp', shift_pairs(1))]
    reduce_sum x114 -> x0, other arithmetic: 335 us -> none  [the longest x32 184 us: local_run(): edge_sum = jnp.sum(edge_lat, axis=1, dtype=jnp.float32).astype(jnp.bfloat16)]
    pallas_call x0 -> x1, Pallas kernels: none -> 285 us  [local_run(): pl.pallas_call(functools.partial(kernel, cfg), out_shape=jax.ShapeDtypeSt...]
    unnamed x471 -> x0, local copies, waits for them, and re-layouts: 275 us -> none
    ppermute x132 -> x0, starting transfers between devices: 273 us -> none  [the longest x32 135 us: local_run(): far_plus = lax.ppermute(mesh_cur, 'gp', shift_pairs(-quarter_hop))]
    another operation x32 -> x0, local copies, waits for them, and re-layouts: 33.6 us -> none  [local_run(): jnp.stack([send_proj[half_shard + 1:half_shard + 1 + mesh_dev], send_proj...]
    convert_element_type x41 -> x0, other arithmetic: 26.7 us -> none  [the longest x38 24.2 us: residual(): return (base.astype(jnp.float32) + update).astype(jnp.bfloat16)]
  transfers between devices with their start and end apart: 132 -> 0, of which waited for: 37 -> 0; matrix products, arithmetic and copies ran while one was open for 12% -> 0% of each run, Pallas kernels for 0% -> 0%
where the time goes in v2:
time: 289 us
  Pallas kernels  285 us (99%)
  local copies, waits for them, and re-layouts  2.95 us (1%)
    pallas_call x1, Pallas kernels, local_run(): pl.pallas_call(functools.partial(kernel, cfg), out_shape=jax.ShapeDtypeSt...  285 us

profile of v2, /device:TPU:21, one launch (start us, length us, event | category | flops | bytes accessed | tf_op | source)
XLA Modules:
  0.0 288.8 jit_solution(7607676062132380046)
XLA Ops:
  0.6 285.2 %shard_map.203 = f32[2,227,1024]{2,1,0:T(8,128)} custom-call(f32[227,1024]{1,0:T(8,128)} %bitcast.17, f32[227,1024]{1,0:T(8,128)} %bitcast.18, f32[5,2,1024]{2,1,0:T(2,128)} %bitcast.21, f32[5,1024]{1,0:T(8,128)} %bitcast.22, f32[4,1024]{1,0:T(4,128)} %bitcast.23, f32[4,1024]{1,0:T(4,128)} %bitcast.24, f32[3,512]{1,0:T(4,128)} %bitcast.25, ...), custom_call_target="tpu_custom_call" | custom-call | tf_op jit(solution)/shard_map/pallas_call | solution.py:606
  285.8 3.0 %slice_bitcast_fusion = (f32[1024,227]{0,1:T(8,128)}, f32[1024,227]{0,1:T(8,128)}) fusion(f32[2,227,1024]{2,1,0:T(8,128)} %shard_map.203), kind=kLoop, calls=%fused_computation | loop fusion | bytes 3719168 | tf_op jit(solution)/shard_map/transpose | solution.py:614

commit v3 on v2

--- a/solution.py
+++ b/solution.py
@@ -13,8 +13,8 @@
 SLAB = 16
 RATIO = 2
 OFFSETS = 6
-LOWER = ("E6", "A7", "S7", "F0", "F1", "A0", "nf1", "E7", "na1", "nf2", "na2", "A1", "ns2", "S0", "F3", "F2", "ne2", "ns1", "ne1", "S1", "E0", "A2", "E1", "S2", "ps2")
-UPPER = ("ro2", "ps1", "E2", "ro1", "pr1", "A3", "S3", "pr2", "F4", "A4", "E3", "F5", "S4", "nf0", "A5", "F6", "na0", "S5", "ns0", "E4", "A6", "ne0", "KEEP", "E5", "S6", "F7", "ps0", "ro0", "pr0")
+LOWER = ("E6", "A7", "S7", "F0", "F1", "A0", "nf1", "E7", "na1", "nf2", "na2", "A1", "ns2", "S0", "F3", "E0", "ne2", "ns1", "F2", "ne1", "S1", "A2", "E1", "S2", "ps2")
+UPPER = ("ro2", "ps1", "E2", "ro1", "pr1", "A3", "S3", "pr2", "F4", "A4", "E3", "F5", "F6", "S4", "nf0", "A5", "na0", "S5", "ns0", "E4", "A6", "ne0", "KEEP", "S6", "E5", "F7", "ps0", "ro0", "pr0")
 
 
 def dot(a, b):
@@ -97,7 +97,10 @@
     for t in range(rows // 128):
         sl = slice(128 * t, 128 * t + 128)
         r.pfwd[sl, :] = onehot(iota((128, rows), 1) == slot_of(iota((128, rows), 0) + 128 * t))
-        r.pbwd[sl, :] = onehot(iota((128, rows), 0) + 128 * t == slot_of(iota((128, rows), 1)))
+        slot = slot_of(iota((128, rows), 1))
+        jp = lax.div(slot, nblk)
+        slot = lax.rem(jp, 2) * (rows // 2) + lax.div(jp, 2) * nblk + lax.rem(slot, nblk)
+        r.pbwd[sl, :] = onehot(iota((128, rows), 0) + 128 * t == slot)
     half = rows // 2
     r.ex[...] = onehot(lax.div(iota((rows, half), 0), RATIO) == iota((rows, half), 1))
     r.ps[...] = onehot(iota((half, rows), 0) == lax.div(iota((half, rows), 1), RATIO))
@@ -236,7 +239,6 @@
         r.encst[pl.ds(base, rows), :] = dot(r.g2m[pl.ds(base, rows), :], r.wi[0, 0:latent, :]) + dot(r.h1[0:rows, :], r.wi[0, 2 * latent:, :])
         return 0
 
-    lax.fori_loop(0, RATIO, g2m_body, 0)
 
     for c in (load.wo0, load.no0, load.wself):
         c.wait()
@@ -273,7 +275,32 @@
         return remote(r.mcur.at[q, pl.ds(pl.multiple_of(nblk * dev, nblk), nblk), :], r.hin.at[2 * owner + q], r.asend.at[off, q], r.arecv.at[off, q], dev)
 
     def to_grid(off, q, dev, owner):
-        return remote(r.yout.at[2 * dev + q], r.hb.at[q, pl.ds(pl.multiple_of(nblk * owner, nblk), nblk), :], r.bsend.at[off, q], r.brecv.at[off, q], dev)
+        return remote(r.yout.at[q, dev], r.hb.at[q, pl.ds(pl.multiple_of(nblk * owner, nblk), nblk), :], r.bsend.at[off, q], r.brecv.at[off, q], dev)
+
+    def encode(q):
+        base = pl.multiple_of(q * rows, rows)
+        at = pl.ds(base, rows)
+        r.p0[...] = dot(r.gl[at, :], r.wi[0, latent:2 * latent, :])
+        act(r.p0, rows, r.h0, lambda o: r.encst[pl.ds(base + o, SLAB), :])
+        r.y0[...] = dot(r.h0[...], r.wo[0])
+
+        def store_edge(o, v):
+            r.h1[o:o + SLAB, :] = (r.g2m[pl.ds(base + o, SLAB), :].astype(F32) + v).astype(BF16)
+
+        finish(r.y0, rows, store_edge)
+        hbase = pl.multiple_of(q * half, half)
+        esum = dot(r.ps[...], r.h1[...]).astype(BF16)
+        r.p1[0:half, :] = dot(esum, r.ni[0, latent:, :])
+        act(r.p1, half, r.h0, lambda o: r.nodst[pl.ds(hbase + o, SLAB), :])
+        r.y1[0:half, :] = dot(r.h0[0:half, :], r.no[0])
+
+        def store_node(o, v):
+            r.mcur[q, o:o + SLAB, :] = (r.mlat[pl.ds(hbase + o, SLAB), :].astype(F32) + v).astype(BF16)
+
+        finish(r.y1, half, store_node)
+        for off in far_first:
+            to_blocks(off, q, lax.rem(me + off, n), me).start()
+        r.hin[2 * me + q] = r.mcur[q, pl.ds(pl.multiple_of(nblk * me, nblk), nblk), :]
 
     s0, sup, sdn, rr, n1, e, h, esum = r.s0, r.sup, r.sdn, r.rr, r.n1, r.e, r.h, r.esum
     npre, nhid, nys = r.np, r.nh, r.ny
@@ -447,38 +474,6 @@
         x_prev, x_cur = r.xs.at[s], r.xs.at[1 - s]
         dmean, dstd = (r.ns[0:nvar, i:i + 1] for i in (2, 3))
 
-        def grid_body(q, _):
-            base = pl.multiple_of(q * rows, rows)
-            at = pl.ds(base, rows)
-
-            @pl.when(s > 0)
-            def _():
-                grid_embed(s, base)
-
-            r.p0[...] = dot(r.gl[at, :], r.wi[0, latent:2 * latent, :])
-            act(r.p0, rows, r.h0, lambda o: r.encst[pl.ds(base + o, SLAB), :])
-            r.y0[...] = dot(r.h0[...], r.wo[0])
-
-            def store_edge(o, v):
-                r.h1[o:o + SLAB, :] = (r.g2m[pl.ds(base + o, SLAB), :].astype(F32) + v).astype(BF16)
-
-            finish(r.y0, rows, store_edge)
-            hbase = pl.multiple_of(q * half, half)
-            esum = dot(r.ps[...], r.h1[...]).astype(BF16)
-            r.p1[0:half, :] = dot(esum, r.ni[0, latent:, :])
-            act(r.p1, half, r.h0, lambda o: r.nodst[pl.ds(hbase + o, SLAB), :])
-            r.y1[0:half, :] = dot(r.h0[0:half, :], r.no[0])
-
-            def store_node(o, v):
-                r.mcur[q, o:o + SLAB, :] = (r.mlat[pl.ds(hbase + o, SLAB), :].astype(F32) + v).astype(BF16)
-
-            finish(r.y1, half, store_node)
-            for off in far_first:
-                to_blocks(off, q, lax.rem(me + off, n), me).start()
-            r.hin[2 * me + q] = r.mcur[q, pl.ds(pl.multiple_of(nblk * me, nblk), nblk), :]
-            return 0
-
-        lax.fori_loop(0, RATIO, grid_body, 0)
         def self_body(q, _):
             base = pl.multiple_of(q * rows, rows)
             at = pl.ds(base, rows)
@@ -509,12 +504,11 @@
 
         run_layers(s * layers)
 
-        r.yout[...] = dot(r.pbwd[...], r.h[...]).astype(BF16).reshape(cols_j, nblk, latent)
         for q in range(2):
+            r.yout[q] = dot(r.pbwd[q * half:(q + 1) * half, :], r.h[...]).astype(BF16).reshape(n, nblk, latent)
             for off in far_first:
                 to_grid(off, q, lax.rem(me + off, n), me).start()
-        for q in range(2):
-            r.hb[q, pl.ds(pl.multiple_of(nblk * me, nblk), nblk), :] = r.yout[2 * me + q]
+            r.hb[q, pl.ds(pl.multiple_of(nblk * me, nblk), nblk), :] = r.yout[q, me]
 
         def dec_body(q, _):
             base = pl.multiple_of(q * rows, rows)
@@ -542,19 +536,36 @@
             act(r.p0, rows, r.h0)
             pred = dot_bt(r.wof[...], r.h0[...])
             x_prev[:, at] = x_cur[:, at] + dstd * pred + dmean
+
+            @pl.when(s == 0)
+            def _():
+                grid_embed(1, base)
+                encode(q)
+
             return 0
 
         lax.fori_loop(0, RATIO, dec_body, 0)
-        pltpu.make_async_copy(x_prev, r.out.at[s], r.out_sem.at[s]).start()
+        for i, out in enumerate((r.out_a, r.out_b)):
+
+            @pl.when(s == i)
+            def _(i=i, out=out):
+                pltpu.make_async_copy(r.xs.at[i], out, r.out_sem.at[i]).start()
+
         return 0
 
     for c in fetch(1, 0):
         c.wait()
     for c in fetch(2, 1):
         c.start()
+    def first_encode(q, _):
+        g2m_body(q, 0)
+        encode(q)
+        return 0
+
+    lax.fori_loop(0, RATIO, first_encode, 0)
     lax.fori_loop(0, 2, step_body, 0)
-    for s in range(2):
-        pltpu.make_async_copy(r.xs.at[s], r.out.at[s], r.out_sem.at[s]).wait()
+    for i, out in enumerate((r.out_a, r.out_b)):
+        pltpu.make_async_copy(r.xs.at[i], out, r.out_sem.at[i]).wait()
     for c in fetch(1, (2 * layers + 1) % 3):
         c.wait()
 
@@ -591,7 +602,7 @@
             m2g=vm((grid_rows, latent), BF16), g2m=vm((grid_rows, latent), BF16), mlat=vm((rows, latent), BF16),
             decst=vm((grid_rows, latent), F32), encst=vm((grid_rows, latent), F32), nodst=vm((rows, latent), F32),
             gl=vm((grid_rows, latent), BF16), gcur=vm((grid_rows, latent), BF16), mcur=vm((2, rows // 2, latent), BF16),
-            hin=vm((cols_j, nblk, latent), BF16), hb=vm((2, rows // 2, latent), BF16), yout=vm((cols_j, nblk, latent), BF16),
+            hin=vm((cols_j, nblk, latent), BF16), hb=vm((2, rows // 2, latent), BF16), yout=vm((2, n, nblk, latent), BF16),
             ebase=vm((OFFSETS * rows, latent), BF16), e=vm((OFFSETS * rows, latent), BF16), h=vm((rows, latent), BF16),
             s0=vm((rows, latent), F32), sup=vm((rows, latent), F32), sdn=vm((rows, latent), F32), rr=vm((rows, latent), F32), n1=vm((rows, latent), F32),
             esum=vm((rows, latent), BF16), edge_s=vm((2, cols_j, latent), F32), keep=vm((cols_j, latent), F32), np=vm((rows, latent), F32), nh=vm((rows, latent), BF16), ny=vm((rows, latent), F32), halo=vm((2, 2, cols_j, latent), F32),
@@ -601,13 +612,13 @@
             load_sem=dma((24,)), fetch_sem=dma((3, 4)), out_sem=dma((2,)), fsend=dma((n, 2)), frecv=dma((n, 2)), nsend=dma((2,)), nrecv=dma((2,)),
             asend=dma((n, 2)), arecv=dma((n, 2)), bsend=dma((n, 2)), brecv=dma((n, 2)), hsend=dma((2,)), hrecv=dma((2, 2)),
         )
-        cfg = types.SimpleNamespace(names=(*inputs, "out", *scratch), n=n, rows=rows, latent=latent, shift=shift, layers=blocks - 2, nvar=nvar, in_feat=in_feat)
+        cfg = types.SimpleNamespace(names=(*inputs, "out_a", "out_b", *scratch), n=n, rows=rows, latent=latent, shift=shift, layers=blocks - 2, nvar=nvar, in_feat=in_feat)
         anywhere = pl.BlockSpec(memory_space=pl.ANY)
         out = pl.pallas_call(
             functools.partial(kernel, cfg),
-            out_shape=jax.ShapeDtypeStruct((2, nvar, grid_rows), F32),
+            out_shape=[jax.ShapeDtypeStruct((nvar, grid_rows), F32)] * 2,
             in_specs=[anywhere] * len(inputs),
-            out_specs=anywhere,
+            out_specs=[anywhere] * 2,
             scratch_shapes=list(scratch.values()),
             compiler_params=pltpu.CompilerParams(collective_id=0, has_side_effects=True, vmem_limit_bytes=66_000_000),
         )(*inputs.values())

time: 289 us -> 283 us (0.979)
  Pallas kernels: 285 us -> 277 us
    pallas_call x1, Pallas kernels: 285 us -> 277 us  [local_run(): pl.pallas_call(functools.partial(kernel, cfg), out_shape=[jax.ShapeDtypeS...]
    unnamed x0 -> x2, local copies, waits for them, and re-layouts: none -> 4.45 us
    transpose x1 -> x0, local copies, waits for them, and re-layouts: 2.95 us -> none  [local_run(): return (out[0].T, out[1].T)]
where the time goes in v3:
time: 283 us
  Pallas kernels  277 us (98%)
  local copies, waits for them, and re-layouts  4.45 us (2%)
    pallas_call x1, Pallas kernels, local_run(): pl.pallas_call(functools.partial(kernel, cfg), out_shape=[jax.ShapeDtypeS...  277 us

profile of v3, /device:TPU:21, one launch (start us, length us, event | category | flops | bytes accessed | tf_op | source)
XLA Modules:
  0.0 282.5 jit_solution(15137009423790697374)
XLA Ops:
  0.6 277.4 %shard_map.203 = (f32[227,1024]{1,0:T(8,128)}, f32[227,1024]{1,0:T(8,128)}) custom-call(f32[227,1024]{1,0:T(8,128)} %bitcast.13, f32[227,1024]{1,0:T(8,128)} %bitcast.14, f32[5,2,1024]{2,1,0:T(2,128)} %bitcast.17, f32[5,1024]{1,0:T(8,128)} %bitcast.18, f32[4,1024]{1,0:T(4,128)} %bitcast.19, f32[4,1024]{1,0:T(4,128)} %bitcast.20, f32[3,512]{1,0:T(4,128)} %bitcast.21, ...), custom_call_target="tpu_custom_call" | custom-call | tf_op jit(solution)/shard_map/pallas_call | solution.py:617
  278.1 2.2 copy.24
  280.3 2.2 copy.25

commit v4 on v3

--- a/solution.py
+++ b/solution.py
@@ -11,6 +11,7 @@
 F32 = jnp.float32
 BF16 = jnp.bfloat16
 SLAB = 16
+GROUP = 64
 RATIO = 2
 OFFSETS = 6
 LOWER = ("E6", "A7", "S7", "F0", "F1", "A0", "nf1", "E7", "na1", "nf2", "na2", "A1", "ns2", "S0", "F3", "E0", "ne2", "ns1", "F2", "ne1", "S1", "A2", "E1", "S2", "ps2")
@@ -94,30 +95,28 @@
         jp = lax.rem(lax.rem(row, cols_j) + (cols_j - 1), cols_j)
         return jp * nblk + lax.rem(lax.div(row, cols_j) + 1, nblk)
 
-    for t in range(rows // 128):
-        sl = slice(128 * t, 128 * t + 128)
-        r.pfwd[sl, :] = onehot(iota((128, rows), 1) == slot_of(iota((128, rows), 0) + 128 * t))
-        slot = slot_of(iota((128, rows), 1))
-        jp = lax.div(slot, nblk)
-        slot = lax.rem(jp, 2) * (rows // 2) + lax.div(jp, 2) * nblk + lax.rem(slot, nblk)
-        r.pbwd[sl, :] = onehot(iota((128, rows), 0) + 128 * t == slot)
     half = rows // 2
     r.ex[...] = onehot(lax.div(iota((rows, half), 0), RATIO) == iota((rows, half), 1))
     r.ps[...] = onehot(iota((half, rows), 0) == lax.div(iota((half, rows), 1), RATIO))
-    for ref in (r.s0, r.sup, r.sdn, r.rr, r.n1, r.edge_s, r.keep, r.esum):
-        ref[...] = jnp.zeros(ref.shape, ref.dtype)
     r.wg[in_feat:, :] = jnp.zeros((r.wg.shape[0] - in_feat, latent), BF16)
 
-    def act(p, count, hidden, add=None):
-        for o in range(0, count, SLAB):
+    def act(p, lo, count, hidden, add=None):
+        for o in range(lo, lo + count, SLAB):
             x = p[o:o + SLAB, :]
             if add is not None:
                 x = x + add(o)
             hidden[o:o + SLAB, :] = silu(x).astype(BF16)
 
-    def finish(y, count, store):
-        for o in range(0, count, SLAB):
-            store(o, layer_norm(y[o:o + SLAB, :]))
+    def finish(y, lo, count, store):
+        for o in range(lo, lo + count, GROUP):
+            store(o, layer_norm(y[o:o + GROUP, :]))
+
+    halves = (0, half)
+
+    def chain(*stages):
+        for stage in stages:
+            for u in halves:
+                stage(slice(u, u + half), u)
 
     st = r.p0
     wide = grid_rows // latent
@@ -159,14 +158,17 @@
         p[2 * nvar:in_feat, :] = r.fs[s, 0:in_feat - 2 * nvar, at]
         p[in_feat:, :] = jnp.zeros((p.shape[0] - in_feat, rows), F32)
         r.h0[...] = p[...].astype(BF16)
-        r.p1[...] = dot_t(r.h0[...], r.wg[...])
-        act(r.p1, rows, r.h1)
-        r.y1[...] = dot(r.h1[...], r.wemb[0])
 
         def store(o, v):
-            r.gl[pl.ds(base + o, SLAB), :] = v.astype(BF16)
-
-        finish(r.y1, rows, store)
+            r.gl[pl.ds(base + o, GROUP), :] = v.astype(BF16)
+
+        def first(w, u):
+            r.p1[w, :] = dot_t(r.h0[:, w], r.wg[...])
+
+        def second(w, u):
+            r.y1[w, :] = dot(r.h1[w, :], r.wemb[0])
+
+        chain(first, lambda w, u: act(r.p1, u, half, r.h1), second, lambda w, u: finish(r.y1, u, half, store))
 
     def first_embed(q, _):
         grid_embed(0, pl.multiple_of(q * rows, rows))
@@ -177,9 +179,8 @@
     lax.fori_loop(0, RATIO, first_embed, 0)
     pl.semaphore_wait(barrier, n - 1)
 
-    def feat_copy(off, jj, dev, owner):
-        slot = lax.rem(2 * owner + jj + cols_j - 1, cols_j)
-        return remote(r.feat.at[jj, pl.ds(pl.multiple_of(nblk * dev, nblk), nblk), :], r.fin.at[slot], r.fsend.at[off, jj], r.frecv.at[off, jj], dev)
+    def feat_copy(off, dev, owner):
+        return remote(r.feat.at[:, pl.ds(pl.multiple_of(nblk * dev, nblk), nblk), :], r.fin.at[pl.ds(2 * owner, 2)], r.fsend.at[off], r.frecv.at[off], dev)
 
     nb_copies = [
         remote(r.mf.at[32:48, 0:half], r.mfp.at[:, half:], r.nsend.at[0], r.nrecv.at[0], left),
@@ -188,19 +189,21 @@
     for c in nb_copies:
         c.start()
     for off in range(1, n):
-        for jj in range(2):
-            feat_copy(off, jj, lax.rem(me + off, n), me).start()
-    for jj in range(2):
-        r.fin[lax.rem(2 * me + jj + cols_j - 1, cols_j)] = r.feat[jj, pl.ds(pl.multiple_of(nblk * me, nblk), nblk), :]
+        feat_copy(off, lax.rem(me + off, n), me).start()
+    r.fin[pl.ds(2 * me, 2)] = r.feat[:, pl.ds(pl.multiple_of(nblk * me, nblk), nblk), :]
     r.mfp[:, 0:half] = r.mf[32:48, half:]
     r.g2p[:, 0:rows] = r.gm[0, :, rows:]
 
 
-    def embed(lhs_t, w_first, w_second, store):
-        r.p0[0:rows, :] = dot_t(lhs_t, w_first)
-        act(r.p0, rows, r.h0)
-        r.y0[0:rows, :] = dot(r.h0[0:rows, :], w_second)
-        finish(r.y0, rows, store)
+    def embed(lhs_t, w_first, w_second, store, last=None):
+        def first(w, u):
+            r.p0[w, :] = dot_t(lhs_t[:, w], w_first)
+
+        def second(w, u):
+            r.y0[w, :] = dot(r.h0[w, :], w_second)
+
+        stages = (first, lambda w, u: act(r.p0, u, half, r.h0), second, lambda w, u: finish(r.y0, u, half, store))
+        chain(*stages, *(() if last is None else (last,)))
 
     load.wi1.wait()
 
@@ -208,10 +211,13 @@
         base = pl.multiple_of(q * rows, rows)
 
         def store(o, v):
-            r.m2g[pl.ds(base + o, SLAB), :] = v.astype(BF16)
-
-        embed(r.gm[1, :, pl.ds(base, rows)], r.ew[2], r.wemb[3], store)
-        r.decst[pl.ds(base, rows), :] = dot(r.m2g[pl.ds(base, rows), :], r.wi[1, 0:latent, :])
+            r.m2g[pl.ds(base + o, GROUP), :] = v.astype(BF16)
+
+        def last(w, u):
+            at = pl.ds(base + u, half)
+            r.decst[at, :] = dot(r.m2g[at, :], r.wi[1, 0:latent, :])
+
+        embed(r.gm[1, :, pl.ds(base, rows)], r.ew[2], r.wemb[3], store, last)
         return 0
 
     lax.fori_loop(0, RATIO, m2g_body, 0)
@@ -222,49 +228,65 @@
     load.ni0.wait()
 
     def store_mesh(o, v):
-        r.mlat[o:o + SLAB, :] = v.astype(BF16)
-
-    embed(r.mfp[...], r.ew[0], r.wemb[1], store_mesh)
-    r.nodst[...] = dot(r.mlat[...], r.ni[0, 0:latent, :])
-
-    def g2m_body(q, _):
+        r.mlat[o:o + GROUP, :] = v.astype(BF16)
+
+    def mesh_last(w, u):
+        r.nodst[w, :] = dot(r.mlat[w, :], r.ni[0, 0:latent, :])
+
+    embed(r.mfp[...], r.ew[0], r.wemb[1], store_mesh, mesh_last)
+
+    def g2m_body(q):
         base = pl.multiple_of(q * rows, rows)
         hbase = pl.multiple_of(q * half, half)
 
         def store(o, v):
-            r.g2m[pl.ds(base + o, SLAB), :] = v.astype(BF16)
-
-        embed(r.g2p[:, pl.ds(base, rows)], r.ew[1], r.wemb[2], store)
-        r.h1[0:rows, :] = dot(r.ex[...], r.mlat[pl.ds(hbase, half), :]).astype(BF16)
-        r.encst[pl.ds(base, rows), :] = dot(r.g2m[pl.ds(base, rows), :], r.wi[0, 0:latent, :]) + dot(r.h1[0:rows, :], r.wi[0, 2 * latent:, :])
-        return 0
-
+            r.g2m[pl.ds(base + o, GROUP), :] = v.astype(BF16)
+
+        def last(w, u):
+            at = pl.ds(base + u, half)
+            r.h1[w, :] = dot(r.ex[0:half, 0:half // 2], r.mlat[pl.ds(hbase + u // 2, half // 2), :]).astype(BF16)
+            r.encst[at, :] = dot(r.g2m[at, :], r.wi[0, 0:latent, :]) + dot(r.h1[w, :], r.wi[0, 2 * latent:, :])
+
+        embed(r.g2p[:, pl.ds(base, rows)], r.ew[1], r.wemb[2], store, last)
 
     for c in (load.wo0, load.no0, load.wself):
         c.wait()
 
     def late_static():
+        for t in range(rows // 128):
+            sl = slice(128 * t, 128 * t + 128)
+            r.pfwd[sl, :] = onehot(iota((128, rows), 1) == slot_of(iota((128, rows), 0) + 128 * t))
+            slot = slot_of(iota((128, rows), 1))
+            jp = lax.div(slot, nblk)
+            slot = lax.rem(jp, 2) * (rows // 2) + lax.div(jp, 2) * nblk + lax.rem(slot, nblk)
+            r.pbwd[sl, :] = onehot(iota((128, rows), 0) + 128 * t == slot)
+        for ref in (r.s0, r.sup, r.sdn, r.rr, r.n1, r.edge_s, r.keep, r.esum):
+            ref[...] = jnp.zeros(ref.shape, ref.dtype)
         for c in (load.wo1, load.ni1, load.no1, load.woh, load.wof):
             c.wait()
         for off in range(1, n):
-            for jj in range(2):
-                feat_copy(off, jj, lax.rem(me + off, n), lax.rem(me + n - off, n)).wait()
-        r.featm[...] = dot(r.pfwd[...], r.fin[...].reshape(rows, 128)).astype(BF16)
+            feat_copy(off, lax.rem(me + off, n), lax.rem(me + n - off, n)).wait()
+        columns = jnp.concatenate([r.fin[1:], r.fin[0:1]], axis=0)
+        r.featm[...] = dot(r.pfwd[...], columns.reshape(rows, 128)).astype(BF16)
 
         def edge_body(k, _):
             sel = onehot(iota((128, 16), 0) == iota((128, 16), 1) + 4 * k)
             sel = jnp.where(iota((128, 16), 1) < 4, sel, jnp.zeros_like(sel))
             w_k = dot(sel, r.ew[3]).astype(BF16)
-            r.p0[0:rows, :] = dot(r.featm[...], w_k)
-            act(r.p0, rows, r.h0)
-            r.y0[0:rows, :] = dot(r.h0[0:rows, :], r.wemb[4])
 
             def store(o, v):
-                pos = flat.index(o // cols_j)
-                at = pl.multiple_of(pos * per_blk + (o % cols_j // SLAB * OFFSETS + k) * SLAB, SLAB)
-                r.ebase[pl.ds(at, SLAB), :] = v.astype(BF16)
-
-            finish(r.y0, rows, store)
+                for i in range(0, GROUP, SLAB):
+                    pos = flat.index((o + i) // cols_j)
+                    at = pl.multiple_of(pos * per_blk + ((o + i) % cols_j // SLAB * OFFSETS + k) * SLAB, SLAB)
+                    r.ebase[pl.ds(at, SLAB), :] = v[i:i + SLAB].astype(BF16)
+
+            def first(w, u):
+                r.p0[w, :] = dot(r.featm[w, :], w_k)
+
+            def second(w, u):
+                r.y0[w, :] = dot(r.h0[w, :], r.wemb[4])
+
+            chain(first, lambda w, u: act(r.p0, u, half, r.h0), second, lambda w, u: finish(r.y0, u, half, store))
             return 0
 
         lax.fori_loop(0, OFFSETS, edge_body, 0)
@@ -279,25 +301,35 @@
 
     def encode(q):
         base = pl.multiple_of(q * rows, rows)
-        at = pl.ds(base, rows)
-        r.p0[...] = dot(r.gl[at, :], r.wi[0, latent:2 * latent, :])
-        act(r.p0, rows, r.h0, lambda o: r.encst[pl.ds(base + o, SLAB), :])
-        r.y0[...] = dot(r.h0[...], r.wo[0])
+        hbase = pl.multiple_of(q * half, half)
+        few = half // RATIO
+
+        def edge_one(w, u):
+            r.p0[w, :] = dot(r.gl[pl.ds(base + u, half), :], r.wi[0, latent:2 * latent, :])
+
+        def edge_two(w, u):
+            r.y0[w, :] = dot(r.h0[w, :], r.wo[0])
 
         def store_edge(o, v):
-            r.h1[o:o + SLAB, :] = (r.g2m[pl.ds(base + o, SLAB), :].astype(F32) + v).astype(BF16)
-
-        finish(r.y0, rows, store_edge)
-        hbase = pl.multiple_of(q * half, half)
-        esum = dot(r.ps[...], r.h1[...]).astype(BF16)
-        r.p1[0:half, :] = dot(esum, r.ni[0, latent:, :])
-        act(r.p1, half, r.h0, lambda o: r.nodst[pl.ds(hbase + o, SLAB), :])
-        r.y1[0:half, :] = dot(r.h0[0:half, :], r.no[0])
+            r.h1[o:o + GROUP, :] = (r.g2m[pl.ds(base + o, GROUP), :].astype(F32) + v).astype(BF16)
+
+        def node_one(w, u):
+            total = dot(r.ps[0:few, 0:half], r.h1[w, :]).astype(BF16)
+            r.p1[u // RATIO:u // RATIO + few, :] = dot(total, r.ni[0, latent:, :])
+
+        def node_two(w, u):
+            at = slice(u // RATIO, u // RATIO + few)
+            r.y1[at, :] = dot(r.h0[at, :], r.no[0])
 
         def store_node(o, v):
-            r.mcur[q, o:o + SLAB, :] = (r.mlat[pl.ds(hbase + o, SLAB), :].astype(F32) + v).astype(BF16)
-
-        finish(r.y1, half, store_node)
+            r.mcur[q, o:o + GROUP, :] = (r.mlat[pl.ds(hbase + o, GROUP), :].astype(F32) + v).astype(BF16)
+
+        chain(
+            edge_one, lambda w, u: act(r.p0, u, half, r.h0, lambda o: r.encst[pl.ds(base + o, SLAB), :]),
+            edge_two, lambda w, u: finish(r.y0, u, half, store_edge),
+            node_one, lambda w, u: act(r.p1, u // RATIO, few, r.h0, lambda o: r.nodst[pl.ds(hbase + o, SLAB), :]),
+            node_two, lambda w, u: finish(r.y1, u // RATIO, few, store_node),
+        )
         for off in far_first:
             to_blocks(off, q, lax.rem(me + off, n), me).start()
         r.hin[2 * me + q] = r.mcur[q, pl.ds(pl.multiple_of(nblk * me, nblk), nblk), :]
@@ -476,16 +508,18 @@
 
         def self_body(q, _):
             base = pl.multiple_of(q * rows, rows)
-            at = pl.ds(base, rows)
-            r.p0[...] = dot(r.gl[at, :], r.wself[0])
-            act(r.p0, rows, r.h0)
-            r.y0[...] = dot(r.h0[...], r.wself[1])
+
+            def first(w, u):
+                r.p0[w, :] = dot(r.gl[pl.ds(base + u, half), :], r.wself[0])
+
+            def second(w, u):
+                r.y0[w, :] = dot(r.h0[w, :], r.wself[1])
 
             def store(o, v):
-                w = pl.ds(base + o, SLAB)
+                w = pl.ds(base + o, GROUP)
                 r.gcur[w, :] = (r.gl[w, :].astype(F32) + v).astype(BF16)
 
-            finish(r.y0, rows, store)
+            chain(first, lambda w, u: act(r.p0, u, half, r.h0), second, lambda w, u: finish(r.y0, u, half, store))
             return 0
 
         lax.fori_loop(0, RATIO, self_body, 0)
@@ -512,30 +546,42 @@
 
         def dec_body(q, _):
             base = pl.multiple_of(q * rows, rows)
-            at = pl.ds(base, rows)
             for off in far_first:
                 to_grid(off, q, lax.rem(me + off, n), lax.rem(me + n - off, n)).wait()
-            r.h1[...] = dot(r.ex[...], r.hb[q]).astype(BF16)
-            r.p0[...] = dot(r.h1[...], r.wi[1, latent:2 * latent, :]) + dot(r.gcur[at, :], r.wi[1, 2 * latent:, :])
-            act(r.p0, rows, r.h0, lambda o: r.decst[pl.ds(base + o, SLAB), :])
-            r.y0[...] = dot(r.h0[...], r.wo[1])
+
+            def edge_one(w, u):
+                r.h1[w, :] = dot(r.ex[0:half, 0:half // RATIO], r.hb[q, u // RATIO:(u + half) // RATIO, :]).astype(BF16)
+                r.p0[w, :] = dot(r.h1[w, :], r.wi[1, latent:2 * latent, :]) + dot(r.gcur[pl.ds(base + u, half), :], r.wi[1, 2 * latent:, :])
+
+            def edge_two(w, u):
+                r.y0[w, :] = dot(r.h0[w, :], r.wo[1])
 
             def store_edge(o, v):
-                r.h1[o:o + SLAB, :] = (r.m2g[pl.ds(base + o, SLAB), :].astype(F32) + v).astype(BF16)
-
-            finish(r.y0, rows, store_edge)
-            r.p1[...] = dot(r.gcur[at, :], r.ni[1, 0:latent, :]) + dot(r.h1[...], r.ni[1, latent:, :])
-            act(r.p1, rows, r.h0)
-            r.y1[...] = dot(r.h0[...], r.no[1])
+                r.h1[o:o + GROUP, :] = (r.m2g[pl.ds(base + o, GROUP), :].astype(F32) + v).astype(BF16)
+
+            def node_one(w, u):
+                r.p1[w, :] = dot(r.gcur[pl.ds(base + u, half), :], r.ni[1, 0:latent, :]) + dot(r.h1[w, :], r.ni[1, latent:, :])
+
+            def node_two(w, u):
+                r.y1[w, :] = dot(r.h0[w, :], r.no[1])
 
             def store_node(o, v):
-                r.h1[o:o + SLAB, :] = (r.gcur[pl.ds(base + o, SLAB), :].astype(F32) + v).astype(BF16)
-
-            finish(r.y1, rows, store_node)
-            r.p0[...] = dot(r.h1[...], r.woh[...])
-            act(r.p0, rows, r.h0)
-            pred = dot_bt(r.wof[...], r.h0[...])
-            x_prev[:, at] = x_cur[:, at] + dstd * pred + dmean
+                r.h1[o:o + GROUP, :] = (r.gcur[pl.ds(base + o, GROUP), :].astype(F32) + v).astype(BF16)
+
+            def out_one(w, u):
+                r.p0[w, :] = dot(r.h1[w, :], r.woh[...])
+
+            def out_two(w, u):
+                at = pl.ds(pl.multiple_of(base + u, half), half)
+                x_prev[:, at] = x_cur[:, at] + dstd * dot_bt(r.wof[...], r.h0[w, :]) + dmean
+
+            chain(
+                edge_one, lambda w, u: act(r.p0, u, half, r.h0, lambda o: r.decst[pl.ds(base + o, SLAB), :]),
+                edge_two, lambda w, u: finish(r.y0, u, half, store_edge),
+                node_one, lambda w, u: act(r.p1, u, half, r.h0),
+                node_two, lambda w, u: finish(r.y1, u, half, store_node),
+                out_one, lambda w, u: act(r.p0, u, half, r.h0), out_two,
+            )
 
             @pl.when(s == 0)
             def _():
@@ -558,7 +604,7 @@
     for c in fetch(2, 1):
         c.start()
     def first_encode(q, _):
-        g2m_body(q, 0)
+        g2m_body(q)
         encode(q)
         return 0
 
@@ -609,7 +655,7 @@
             p0=vm((big, latent), F32), p1=vm((big, latent), F32), h0=vm((big, latent), BF16), h1=vm((big, latent), BF16), y0=vm((big, latent), F32), y1=vm((big, latent), F32),
             wof=vm((nvar, latent), BF16), mfr=vm((mesh_feat.shape[1], rows), F32), mer=vm((*mesh_edge_feat.shape[1:], rows), F32), g2r=vm((g2m_feat.shape[1], grid_rows), F32), m2r=vm((m2g_feat.shape[1], grid_rows), F32),
             gsr=vm((grid_static.shape[1], grid_rows), F32), frr=vm((forcing.shape[2], forcing.shape[1], grid_rows), F32), nsr=vm(norm_stats.shape, F32), wmr=vm(w_mesh_in.shape, BF16), wer=vm(w_eemb_in.shape, BF16),
-            load_sem=dma((24,)), fetch_sem=dma((3, 4)), out_sem=dma((2,)), fsend=dma((n, 2)), frecv=dma((n, 2)), nsend=dma((2,)), nrecv=dma((2,)),
+            load_sem=dma((24,)), fetch_sem=dma((3, 4)), out_sem=dma((2,)), fsend=dma((n,)), frecv=dma((n,)), nsend=dma((2,)), nrecv=dma((2,)),
             asend=dma((n, 2)), arecv=dma((n, 2)), bsend=dma((n, 2)), brecv=dma((n, 2)), hsend=dma((2,)), hrecv=dma((2, 2)),
         )
         cfg = types.SimpleNamespace(names=(*inputs, "out_a", "out_b", *scratch), n=n, rows=rows, latent=latent, shift=shift, layers=blocks - 2, nvar=nvar, in_feat=in_feat)

time: 283 us -> 283 us (level)
  no operation moved by 1% of the time
where the time goes in v4:
time: 283 us; the launch traced here: 282 us
  Pallas kernels  277 us (98%)
  local copies, waits for them, and re-layouts  4.45 us (2%)
    pallas_call x1, Pallas kernels, local_run(): pl.pallas_call(functools.partial(kernel, cfg), out_shape=[jax.ShapeDtypeS...  277 us

profile of v4, /device:TPU:21, one launch (start us, length us, event | category | flops | bytes accessed | tf_op | source)
XLA Modules:
  0.0 282.5 jit_solution(10968187714131771193)
XLA Ops:
  0.6 277.4 %shard_map.203 = (f32[227,1024]{1,0:T(8,128)}, f32[227,1024]{1,0:T(8,128)}) custom-call(f32[227,1024]{1,0:T(8,128)} %bitcast.13, f32[227,1024]{1,0:T(8,128)} %bitcast.14, f32[5,2,1024]{2,1,0:T(2,128)} %bitcast.17, f32[5,1024]{1,0:T(8,128)} %bitcast.18, f32[4,1024]{1,0:T(4,128)} %bitcast.19, f32[4,1024]{1,0:T(4,128)} %bitcast.20, f32[3,512]{1,0:T(4,128)} %bitcast.21, ...), custom_call_target="tpu_custom_call" | custom-call | tf_op jit(solution)/shard_map/pallas_call | solution.py:663
  278.0 2.2 copy.24
  280.3 2.2 copy.25
